TPU v7x, 128 devices: a whole 4x4x4 slice. The times are simulated.
128 devices in a mesh: row: 8 (over z, y_hi), col: 16 (over y_lo, x, core).
Axes of the slice: x: 4, y: 4 (y_hi: 2, y_lo: 2; y = y_hi * 2 + y_lo), z: 4, core: 2. Of those that a mesh axis runs over, the one named last changes fastest.
Arguments:
- green: float32 [2048, 16384], P(('row', 'col')), may hold values from -0.1875 to 0.1875
- noise_precision: float32 [2048], P(('row', 'col')), may hold values from 0.5 to 4
- data_set: int32 [2048], P(('row', 'col')), may hold values from 0 to 3
- set_scale: float32 [4], replicated, may hold values from 0.5 to 2
- stiffness: float32 [8192], replicated, may hold values from 0.25 to 2
- patch_cell: int32 [8192], replicated, may hold values from 0 to 8191, each once
Outputs:
- precision_matrix: float32 [16384, 16384], P('row', 'col')
Inputs may be any that keep to these rules, and one draw needn't show every extreme that they name: `patch_cell`: every cell 0 to 8191 holds exactly one patch.
All inputs are finite; a program needn't handle non-finite values.
Results may differ from a plain program's by a relative error of at most 0.00005.
Values sent between devices are 32-bit elements; how exact they have to be, the bound alone decides.
No kernel may reach another device: no remote copies, remote signals or barrier semaphores. Data moves between devices by JAX's collectives and lax.ppermute only.
A program may use at most 256 MiB of HBM per device.

v0:
```python
import jax
import jax.numpy as jnp
from jax import lax
from jax.sharding import PartitionSpec as P

NSTRIKE = 128
NDIP = 64


def gram_product(left_panel, right_panel):
    return lax.dot_general(
        left_panel,
        right_panel,
        (((0,), (0,)), ((), ())),
        precision=lax.Precision.HIGHEST,
        preferred_element_type=jnp.float32,
    )


def degree_table(stiffness, patch_cell):
    sorted_cells, cell_stiff = lax.sort_key_val(patch_cell, stiffness)
    grid = cell_stiff.reshape(NSTRIKE, NDIP)
    padded = jnp.pad(grid, 1)
    strike_ids = lax.broadcasted_iota(jnp.int32, (NSTRIKE, NDIP), 0)
    dip_ids = lax.broadcasted_iota(jnp.int32, (NSTRIKE, NDIP), 1)
    degree = jnp.zeros((NSTRIKE, NDIP), jnp.float32)
    degree = degree + jnp.where(strike_ids < NSTRIKE - 1, 0.5 * (grid + padded[2:, 1:-1]), 0.0)
    degree = degree + jnp.where(strike_ids > 0, 0.5 * (grid + padded[:-2, 1:-1]), 0.0)
    degree = degree + jnp.where(dip_ids < NDIP - 1, 0.5 * (grid + padded[1:-1, 2:]), 0.0)
    degree = degree + jnp.where(dip_ids > 0, 0.5 * (grid + padded[1:-1, :-2]), 0.0)
    return degree.reshape(NSTRIKE * NDIP)


def smoothing_tile(stiffness, patch_cell, row_start, tile_height, col_start, tile_width):
    patch_count = stiffness.shape[0]
    degree_cells = degree_table(stiffness, patch_cell)
    row_first = row_start % patch_count
    col_first = col_start % patch_count
    row_cell = lax.dynamic_slice_in_dim(patch_cell, row_first, tile_height, 0)
    col_cell = lax.dynamic_slice_in_dim(patch_cell, col_first, tile_width, 0)
    row_stiff = lax.dynamic_slice_in_dim(stiffness, row_first, tile_height, 0)
    col_stiff = lax.dynamic_slice_in_dim(stiffness, col_first, tile_width, 0)
    row_degree = jnp.take(degree_cells, row_cell)
    row_strike = row_cell // NDIP
    row_dip = row_cell % NDIP
    col_strike = col_cell // NDIP
    col_dip = col_cell % NDIP
    spacing = jnp.abs(row_strike[:, None] - col_strike[None, :]) + jnp.abs(
        row_dip[:, None] - col_dip[None, :]
    )
    row_ids = row_start + jnp.arange(tile_height, dtype=jnp.int32)
    col_ids = col_start + jnp.arange(tile_width, dtype=jnp.int32)
    same_part = row_ids[:, None] // patch_count == col_ids[None, :] // patch_count
    coupling = jnp.where(
        (spacing == 1) & same_part, -0.5 * (row_stiff[:, None] + col_stiff[None, :]), 0.0
    )
    diagonal = row_ids[:, None] == col_ids[None, :]
    return coupling + jnp.where(diagonal, row_degree[:, None], 0.0)


def per_device(green, noise_precision, data_set, set_scale, stiffness, patch_cell):
    row_count = lax.axis_size("row")
    col_count = lax.axis_size("col")
    local_rows = green.shape[0]
    order_full = green.shape[1]
    tile_height = order_full // row_count
    tile_width = order_full // col_count
    matches = data_set[:, None] == jnp.arange(set_scale.shape[0], dtype=jnp.int32)[None, :]
    weight = noise_precision * jnp.sum(jnp.where(matches, set_scale[None, :], 0.0), axis=1)
    scaled = green * jnp.sqrt(weight)[:, None]
    by_column = lax.all_to_all(scaled, "col", split_axis=1, concat_axis=0, tiled=True)
    right_factor = lax.all_gather(by_column, "row", axis=0, tiled=True)
    by_row = lax.all_to_all(scaled, "row", split_axis=1, concat_axis=0, tiled=True)
    reordered = jnp.transpose(
        right_factor.reshape(row_count, col_count, local_rows, tile_width), (1, 0, 2, 3)
    ).reshape(row_count * col_count * local_rows, tile_width)
    gram_tile = gram_product(lax.all_gather(by_row, "col", axis=0, tiled=True), reordered)
    prior = smoothing_tile(
        stiffness,
        patch_cell,
        lax.axis_index("row") * tile_height,
        tile_height,
        lax.axis_index("col") * tile_width,
        tile_width,
    )
    return gram_tile + prior


def solution(mesh):
    placed = (P(("row", "col"), None), P(("row", "col")), P(("row", "col")), P(), P(), P())
    return jax.shard_map(
        per_device, mesh=mesh, in_specs=placed, out_specs=P("row", "col"), check_vma=False
    )
```

profile of v0, /device:TPU:1, one launch (start us, length us, event | category | flops | bytes accessed | tf_op | source)
XLA Modules:
  0.0 306.4 jit_solution(10095303968198410962)
XLA Ops:
  6.5 0.0 all-gather.5.cloned.1.call-start
  6.5 0.8 select_reduce_fusion
  7.3 0.7 multiply_sqrt_fusion
  8.0 1.4 broadcast_multiply_fusion
  9.3 0.1 copy.21
  9.4 21.8 %all_to_all.38 = f32[16,16,1024]{2,0,1:T(8,128)} all-to-all(f32[16,16,1024]{2,0,1:T(8,128)S(1)} %bitcast.27), channel_id=1, replica_groups=mesh['row'=8,'col'=16] {'col'}, dimensions={1} | all-to-all | bytes 2097152 | tf_op jit(solution)/shard_map/all_to_all | solution.py:71
  31.2 0.0 all-gather.5.cloned.1.call-update
  31.3 0.0 all-gather.3.cloned.1.call-start
  31.3 0.1 copy.22
  31.4 27.9 %all_to_all.39 = f32[16,8,2048]{2,0,1:T(8,128)} all-to-all(f32[16,8,2048]{2,0,1:T(8,128)S(1)} %bitcast.26), channel_id=1, replica_groups=mesh['row'=8,'col'=16] {'row'}, dimensions={1} | all-to-all | bytes 2097152 | tf_op jit(solution)/shard_map/all_to_all | solution.py:73
  59.3 0.0 all-gather.3.cloned.1.call-update
  59.4 0.0 copy-done.1
  59.4 0.0 copy-done
  59.4 6.9 %sort.23 = (s32[8192]{0:T(1024)}, f32[8192]{0:T(1024)S(1)}, s32[8192]{0:T(1024)}) sort(s32[8192]{0:T(1024)S(1)} %copy-done, f32[8192]{0:T(1024)S(1)} %copy-done.1, s32[8192]{0:T(1024)S(1)} %iota.45), dimensions={0}, to_apply=%region_1.2 | sort | flops 106496 | bytes 196608 | tf_op jit(solution)/shard_map/sort | solution.py:21
  66.3 0.1 reshape.114
  66.4 0.1 select_add_fusion
  66.6 0.1 reshape.115
  66.7 11.8 %gather_fusion = f32[2048]{0:T(1024)S(1)} fusion(f32[8192]{0:T(1024)S(1)} %reshape.115, s32[2048]{0:T(1024)S(1)} %get-tuple-element.14), kind=kCustom, calls=%fused_computation | custom fusion | bytes 24576 | tf_op jit(solution)/shard_map/jit(_take)/gather | solution.py:43
  78.6 65.3 %all-gather.5.cloned.1.call-done = f32[2048,1024]{1,0:T(8,128)} async-done(((f32[256,1024]{1,0:T(8,128)}), f32[2048,1024]{1,0:T(8,128)}) %all-gather.5.cloned.1.call-update) | async-done | bytes 8388624 | tf_op jit(solution)/shard_map/all_gather | solution.py:72
  143.9 8.3 %copy.16 = f32[8,16,16,1024]{3,2,0,1:T(8,128)} copy(f32[8,16,16,1024]{3,2,1,0:T(8,128)} %bitcast.22) | data formatting | bytes 16777216 | tf_op jit(solution)/shard_map/reshape | solution.py:75
  152.2 83.8 %all-gather.3.cloned.1.call-done = f32[2048,2048]{1,0:T(8,128)} async-done(((f32[128,2048]{1,0:T(8,128)}), f32[2048,2048]{1,0:T(8,128)}) %all-gather.3.cloned.1.call-update) | async-done | bytes 16777232 | tf_op jit(solution)/shard_map/all_gather | solution.py:77
  236.0 0.0 dynamic-slice-done
  236.0 0.0 dynamic-slice-done.1
  236.0 63.5 %add_add_fusion = f32[2048,1024]{1,0:T(8,128)} fusion(f32[2048]{0:T(1024)S(1)} %and_select_fusion, s32[1024]{0:T(1024)S(1)} %get-tuple-element.22, f32[1024]{0:T(1024)S(1)} %dynamic-slice-done, f32[2048]{0:T(1024)S(1)} %dynamic-slice-done.1, s32[1024]{0:T(1024)S(1)} %get-tuple-element.21, s32[1024]{0:T(1024)S(1)} %add_select_fusion.5, ...), kind=kOutput, calls=%fused_computation.1 | convolution fusion | flops 51571064832 | bytes 33624064 | tf_op jit(solution)/shard_map/dot_general | solution.py:11
  (14 shorter events, 0.1 us)
Async XLA Ops:
  6.5 52.9 %copy-start.1 = (f32[8192]{0:T(1024)S(1)}, f32[8192]{0:T(1024)}, u32[]{:S(2)}) copy-start(f32[8192]{0:T(1024)} %param.10) | copy-start | bytes 98308
  6.5 52.9 %copy-start = (s32[8192]{0:T(1024)S(1)}, s32[8192]{0:T(1024)}, u32[]{:S(2)}) copy-start(s32[8192]{0:T(1024)} %param.11) | copy-start | bytes 98308
  6.5 137.3 %all-gather.5.cloned.1.call-start = ((), (), s32[]{:S(2)}) async-start(), calls=%async_computation.3 | async-start | bytes 9437184 | tf_op jit(solution)/shard_map/all_gather | solution.py:72
  31.3 204.7 %all-gather.3.cloned.1.call-start = ((), (), s32[]{:S(2)}) async-start(), calls=%async_computation.2 | async-start | bytes 17825792 | tf_op jit(solution)/shard_map/all_gather | solution.py:77
  143.9 92.1 %dynamic-slice-start = ((f32[8192]{0:T(1024)}, s32[]{:T(128)}), f32[1024]{0:T(1024)S(1)}, s32[]{:S(2)}) async-start(f32[8192]{0:T(1024)} %param.10, s32[]{:T(128)} %select_n.101), calls=%async_computation.4 | async-start | bytes 8704 | tf_op jit(solution)/shard_map/dynamic_slice | solution.py:42
  143.9 92.1 %dynamic-slice-start.1 = ((f32[8192]{0:T(1024)}, s32[]{:T(128)}), f32[2048]{0:T(1024)S(1)}, s32[]{:S(2)}) async-start(f32[8192]{0:T(1024)} %param.10, s32[]{:T(128)} %select_n.98), calls=%async_computation.5 | async-start | bytes 16896 | tf_op jit(solution)/shard_map/dynamic_slice | solution.py:41
Sparse Core Ops, SparseCore 0:
  31.4 112.4 all-gather.4
  145.6 90.3 all-gather.2
where the time goes:
time: 307 us; the launch traced here: 306 us
  waiting for transfers between devices  149 us (49%)
  matrix products  63.5 us (21%)
  blocking collectives  49.8 us (16%)
  local copies, waits for them, and re-layouts  20.4 us (7%)
  between operations  13.6 us (4%)
  other arithmetic  9.95 us (3%)
    all_gather x1, waiting for transfers between devices, per_device(): lax.all_gather(by_row, 'col', axis=0, tiled=True)  83.8 us
    all_gather x1, waiting for transfers between devices, per_device(): right_factor = lax.all_gather(by_column, 'row', axis=0, tiled=True)  65.3 us
    dot_general x1, matrix products, gram_product(): lax.dot_general(left_panel, right_panel, (((0,), (0,)), ((), ())), precis...  63.5 us
    all_to_all x1, blocking collectives, per_device(): lax.all_to_all(scaled, 'row', split_axis=1, concat_axis=0, tiled=True)  27.9 us
    all_to_all x1, blocking collectives, per_device(): lax.all_to_all(scaled, 'col', split_axis=1, concat_axis=0, tiled=True)  21.8 us
    gather x1, local copies, waits for them, and re-layouts, smoothing_tile(): row_degree = jnp.take(degree_cells, row_cell)  11.8 us
    reshape x1, local copies, waits for them, and re-layouts, per_device(): right_factor.reshape(row_count, col_count, local_rows, tile_width)  8.3 us
    sort x1, other arithmetic, degree_table(): sorted_cells, cell_stiff = lax.sort_key_val(patch_cell, stiffness)  6.9 us
  transfers between devices with their start and end apart: 2, of which 2 were waited for; matrix products, arithmetic and copies ran while one was open for 9% of the time, Pallas kernels for 0%

commit v1 on v0

v1 whole, which is shorter than its diff:
```python
import functools

import jax
import jax.numpy as jnp
from jax import lax
from jax.experimental import pallas as pl
from jax.experimental.pallas import tpu as pltpu
from jax.sharding import PartitionSpec as P


NSTRIKE = 128
NDIP = 64
AXES = ("row", "col")
CROSS = (3, 2, 1, 0)
PAIR = (1, 0, 3, 2)
DIAGONAL = (2, 3, 0, 1)
ROWS = 2048
COLS = 1024
PATCHES = 8192


def place(index):
    row, col = divmod(index, 16)
    z, y_hi = divmod(row, 2)
    y_lo, rest = divmod(col, 8)
    x, core = divmod(rest, 2)
    return z, 2 * y_hi + y_lo, x, core


def device(z, y, x, core):
    return (z % 4 * 2 + y // 2) * 16 + (y % 2) * 8 + x % 4 * 2 + core


def send(block, target):
    pairs = [(index, device(*target(*place(index)))) for index in range(128)]
    return lax.ppermute(block, AXES, pairs)


def kernel_call(body, outs, args, in_specs=None, flops=0, nbytes=0, scratch=(), limit=6, **extra):
    return pl.pallas_call(
        body,
        out_shape=outs,
        in_specs=in_specs or [VMEM] * len(args),
        scratch_shapes=scratch,
        cost_estimate=pl.CostEstimate(flops=flops, bytes_accessed=nbytes, transcendentals=0),
        compiler_params=pltpu.CompilerParams(vmem_limit_bytes=limit << 20),
        **extra,
    )(*args)


def shape(*dims):
    return jax.ShapeDtypeStruct(dims, jnp.float32)


VMEM = pl.BlockSpec(memory_space=pltpu.VMEM)
SMEM = pl.BlockSpec(memory_space=pltpu.SMEM)


def scale_body(spot, scales, green, noise, sets, *outs):
    row_pieces, mine, theirs = outs[:8], outs[8], outs[9]
    z, y_hi, y_lo, x, core = (spot[i] for i in range(5))
    chosen = sets[...]
    factor = jnp.zeros_like(noise[...])
    for s in range(4):
        factor = jnp.where(chosen == s, scales[s], factor)
    root = jnp.broadcast_to(jnp.sqrt(noise[...] * factor), (16, 16))
    eye = lax.broadcasted_iota(jnp.int32, (16, 16), 0) == lax.broadcasted_iota(jnp.int32, (16, 16), 1)
    root = jnp.sum(jnp.where(eye, root, 0.0), axis=1, keepdims=True)
    for c in range(2):
        hi = y_hi if c == 0 else 1 - y_hi
        lo = y_lo if c == 0 else 1 - y_lo
        for d in range(4):
            start = (lax.rem(z + d, 4) * 2 + hi) * 2048
            row_pieces[c * 4 + d][...] = green[:, pl.ds(pl.multiple_of(start, 2048), 2048)] * root
            start = (lo * 4 + lax.rem(x + d, 4)) * 2048
            mine[c * 4 + d] = green[:, pl.ds(pl.multiple_of(start + core * 1024, 1024), 1024)] * root
            theirs[c * 4 + d] = green[:, pl.ds(pl.multiple_of(start + (1 - core) * 1024, 1024), 1024)] * root


def split_body(mine, other, *outs):
    for i in range(8):
        outs[i][0] = mine[i]
        outs[i][1] = other[i]


def join_rows_body(*refs):
    out = refs[8]
    for c in range(2):
        for d in range(4):
            out[(d * 2 + c) * 16 : (d * 2 + c + 1) * 16, :] = refs[c * 4 + d][...]


def join_cols_body(*refs):
    out = refs[8]
    for c in range(2):
        for d in range(4):
            for j in range(2):
                at = ((d * 2 + c) * 2 + j) * 16
                out[at : at + 16, :] = refs[c * 4 + d][j]


def exact(left, right, dims):
    return lax.dot_general(
        left, right, (dims, ((), ())), precision=lax.Precision.HIGHEST, preferred_element_type=jnp.float32
    )


def sides_body(spot, cell, stiff, row_side, col_side):
    grid = jnp.zeros((NSTRIKE, NDIP), jnp.float32)
    for i in range(8):
        part = pl.ds(i * 1024, 1024)
        cells = cell[:, part]
        strikes = lax.broadcasted_iota(jnp.int32, (NSTRIKE, 1024), 0)
        dips = lax.broadcasted_iota(jnp.int32, (NDIP, 1024), 0)
        at_strike = jnp.where(cells // NDIP == strikes, stiff[:, part], 0.0)
        at_dip = jnp.where(cells % NDIP == dips, 1.0, 0.0)
        grid = grid + exact(at_strike, at_dip, ((1,), (1,)))
    along = jnp.zeros((1, NDIP), jnp.float32)
    across = jnp.zeros((NSTRIKE, 1), jnp.float32)
    strike_ids = lax.broadcasted_iota(jnp.int32, (NSTRIKE, NDIP), 0)
    dip_ids = lax.broadcasted_iota(jnp.int32, (NSTRIKE, NDIP), 1)
    after = jnp.concatenate([grid[1:], along], 0)
    before = jnp.concatenate([along, grid[:-1]], 0)
    below = jnp.concatenate([grid[:, 1:], across], 1)
    above = jnp.concatenate([across, grid[:, :-1]], 1)
    degree = jnp.where(strike_ids < NSTRIKE - 1, 0.5 * (grid + after), 0.0)
    degree = degree + jnp.where(strike_ids > 0, 0.5 * (grid + before), 0.0)
    degree = degree + jnp.where(dip_ids < NDIP - 1, 0.5 * (grid + below), 0.0)
    degree = degree + jnp.where(dip_ids > 0, 0.5 * (grid + above), 0.0)
    first = pl.multiple_of(spot[5], 2048)
    cells = cell[:, pl.ds(first, ROWS)]
    strike = cells // NDIP
    dip = cells % NDIP
    in_strike = jnp.where(strike == lax.broadcasted_iota(jnp.int32, (NSTRIKE, ROWS), 0), 1.0, 0.0)
    by_dip = exact(degree.T, in_strike, ((1,), (0,)))
    in_dip = dip == lax.broadcasted_iota(jnp.int32, (NDIP, ROWS), 0)
    row_degree = jnp.sum(jnp.where(in_dip, by_dip, 0.0), axis=0, keepdims=True)
    row_side[0:1, :] = strike.astype(jnp.float32)
    row_side[1:2, :] = dip.astype(jnp.float32)
    row_side[2:3, :] = 0.5 * stiff[:, pl.ds(first, ROWS)]
    row_side[3:4, :] = row_degree
    row_side[4:8, :] = jnp.zeros((4, ROWS), jnp.float32)
    first = pl.multiple_of(spot[6], 1024)
    cells = cell[:, pl.ds(first, COLS)]
    col_side[0:1, :] = (cells // NDIP).astype(jnp.float32)
    col_side[1:2, :] = (cells % NDIP).astype(jnp.float32)
    col_side[2:3, :] = 0.5 * stiff[:, pl.ds(first, COLS)]
    col_side[3:8, :] = jnp.zeros((5, COLS), jnp.float32)


def prior_tile(spot, row_side, col_side):
    sides = row_side.T
    spacing = jnp.abs(sides[:, 0:1] - col_side[0:1, :]) + jnp.abs(sides[:, 1:2] - col_side[1:2, :])
    spacing = jnp.where(spot[7] == 1, spacing, 9.0)
    coupling = jnp.where(spacing == 1.0, -(sides[:, 2:3] + col_side[2:3, :]), 0.0)
    return jnp.where(spacing == 0.0, sides[:, 3:4], coupling)


def split_right(late, core, right, spots, high, low):
    depth = 32 * len(right)
    for n in range(4):
        for j in range(2):
            who = core if j == 0 else 1 - core
            dx = (0, 1 + 2 * who, 3 - 2 * who, 2)[n]
            for ref, at in zip(right, spots):
                for c in range(2):
                    c_from = 1 - c if late else c
                    source = pl.multiple_of(dx * 64 + c_from * 32 + j * 16, 16)
                    target = pl.multiple_of((j * 4 + n) * depth + at * 32 + c * 16, 16)
                    piece = ref[pl.ds(source, 16), :]
                    top = piece.astype(jnp.bfloat16)
                    high[pl.ds(target, 16), :] = top
                    low[pl.ds(target, 16), :] = (piece - top.astype(jnp.float32)).astype(jnp.bfloat16)


def product(left, rows, part, high, low):
    block = jnp.concatenate([ref[a:b, part] for ref in left for a, b in rows], 0).T
    top = block.astype(jnp.bfloat16)
    rest = (block - top.astype(jnp.float32)).astype(jnp.bfloat16)

    def dot(a, b):
        return jnp.dot(a, b, preferred_element_type=jnp.float32)

    return dot(top, high[...]) + (dot(top, low[...]) + dot(rest, high[...]))


ALL = ((0, 128),)
MOST = ((0, 64), (96, 128))
FAR = ((64, 96),)


def near_body(start, stop, spot, *refs):
    left, right = refs[:8], refs[8:12]
    row_side, col_side = refs[12:14]
    out, high, low = refs[-3:]
    core = spot[4]
    split_right(False, core, right, (0, 1 + 2 * core, 3 - 2 * core, 2), high, low)

    @pl.loop(start // TILE, stop // TILE)
    def _(i):
        part = pl.ds(pl.multiple_of(i * TILE, TILE), TILE)
        out[part, :] = product(left, ALL, part, high, low) + prior_tile(spot, row_side[:, part], col_side)


def late_body(spot, *refs):
    left, right = refs[:8], refs[8:11]
    total, out, high, low = refs[11:]
    core = spot[4]
    split_right(True, core, right, (0, 1 + core, 2 - core), high, low)

    @pl.loop(0, ROWS // TILE)
    def _(i):
        part = pl.ds(pl.multiple_of(i * TILE, TILE), TILE)
        out[part, :] = total[part, :] + product(left, MOST, part, high, low)


def far_body(spot, *refs):
    left, right = refs[:8], refs[8:9]
    total, out, high, low = refs[9:]

    @pl.when(pl.program_id(0) == 0)
    def _():
        split_right(True, spot[4], right, (0,), high, low)

    part = pl.ds(pl.multiple_of(pl.program_id(0) * TILE, TILE), TILE)
    out[...] = total[part, :] + product(left, FAR, part, high, low)


TILE = 256


def gram_call(body, depth, spot, *args, **extra):
    args = (spot, *args)
    return kernel_call(
        body,
        shape(ROWS, COLS),
        args,
        in_specs=[SMEM] + [VMEM] * (len(args) - 1),
        scratch=[pltpu.VMEM((depth, COLS), jnp.bfloat16)] * 2,
        flops=3 * 2 * ROWS * COLS * depth,
        nbytes=24 << 20,
        limit=12,
        **extra,
    )


def ring(block, axis):
    def shift(sign):
        def target(z, y, x, core):
            step = sign if core == 0 else -sign
            return (z + step, y, x, core) if axis == "z" else (z, y, x + step, core)

        return target

    first = send(block, shift(1))
    second = send(block, shift(-1))
    far = send(first, shift(1))
    return [block, first, second, far]


def swap(blocks):
    return [send(b, lambda z, y, x, core: (z, y, x, 1 - core)) for b in blocks]


def scatter(pieces, axis):
    got = []
    for c in range(2):
        for d in range(4):
            if c == 0 and d == 0:
                got.append(pieces[0])
                continue

            def target(z, y, x, core):
                to = CROSS[y] if c else y
                return (z + d, to, x, core) if axis == "z" else (z, to, x + d, core)

            got.append(send(pieces[c * 4 + d], target))
    return got


def per_device(green, noise_precision, data_set, set_scale, stiffness, patch_cell):
    row, col = lax.axis_index("row"), lax.axis_index("col")
    row_start, col_start = row * ROWS, col * COLS
    spot = jnp.stack(
        [
            row // 2,
            row % 2,
            col // 8,
            col // 2 % 4,
            col % 2,
            row_start % PATCHES,
            col_start % PATCHES,
            (row_start // PATCHES == col_start // PATCHES).astype(jnp.int32),
        ]
    ).astype(jnp.int32)
    *row_pieces, mine, theirs = kernel_call(
        scale_body,
        [shape(16, 2048)] * 8 + [shape(8, 16, 1024)] * 2,
        (spot, set_scale, green, noise_precision.reshape(1, 16), data_set.reshape(1, 16)),
        in_specs=[SMEM, SMEM, VMEM, VMEM, VMEM],
        flops=1 << 20,
        nbytes=3 << 20,
    )
    (other,) = swap([theirs])
    row_pieces = scatter(row_pieces, "z")
    col_pieces = kernel_call(split_body, [shape(2, 16, 1024)] * 8, (mine, other), flops=1 << 20, nbytes=2 << 20)
    col_pieces = scatter(col_pieces, "x")
    row_near = kernel_call(join_rows_body, shape(128, 2048), row_pieces, flops=1 << 20, nbytes=2 << 20)
    row_late = send(row_near, lambda z, y, x, core: (z, PAIR[y], x, core))
    col_near = kernel_call(join_cols_body, shape(256, 1024), col_pieces, flops=1 << 20, nbytes=2 << 20)
    col_late = send(col_near, lambda z, y, x, core: (z, DIAGONAL[y], x, core))
    sides = kernel_call(
        sides_body,
        [shape(8, ROWS), shape(8, COLS)],
        (spot, patch_cell.reshape(1, -1), stiffness.reshape(1, -1)),
        in_specs=[SMEM, VMEM, VMEM],
        flops=1 << 30,
        nbytes=1 << 20,
    )
    row_near = ring(row_near, "x")
    col_near = ring(col_near, "z")
    row_late = ring(row_late, "x")
    col_late = ring(col_late, "z")
    left = row_near + swap(row_near)
    total = gram_call(functools.partial(near_body, 0, ROWS // 2), 1024, spot, *left, *col_near, *sides)
    total = gram_call(
        functools.partial(near_body, ROWS // 2, ROWS),
        1024,
        spot,
        *left,
        *col_near,
        *sides,
        total,
        input_output_aliases={15: 0},
    )
    left = row_late + swap(row_late)
    total = gram_call(late_body, 768, spot, *left, *col_late[:3], total, input_output_aliases={12: 0})
    return gram_call(
        far_body,
        256,
        spot,
        *left,
        col_late[3],
        total,
        grid=(ROWS // TILE,),
        out_specs=pl.BlockSpec((TILE, COLS), lambda i: (i, 0)),
    )


def solution(mesh):
    placed = (P(AXES, None), P(AXES), P(AXES), P(), P(), P())

    return jax.shard_map(per_device, mesh=mesh, in_specs=placed, out_specs=P("row", "col"), check_vma=False)
```

time: 307 us -> 193 us (0.63)
  waiting for transfers between devices: 149 us -> 69.5 us
  starting transfers between devices: 0.04 us -> 73.1 us
  matrix products: 63.5 us -> 0 us
  blocking collectives: 49.8 us -> 0 us
  Pallas kernels: 0 us -> 45.3 us
  local copies, waits for them, and re-layouts: 20.4 us -> 4.79 us
  between operations: 13.6 us -> 0.16 us
  other arithmetic: 9.95 us -> 0 us
    all_gather x2 -> x0, waiting for transfers between devices: 149 us -> none  [the longest x1 83.8 us: per_device(): lax.all_gather(by_row, 'col', axis=0, tiled=True)]
    ppermute x0 -> x37, starting transfers between devices: none -> 73.1 us  [send(): return lax.ppermute(block, AXES, pairs)]
    ppermute x0 -> x37, waiting for transfers between devices: none -> 69.5 us  [send(): return lax.ppermute(block, AXES, pairs)]
    dot_general x1 -> x0, matrix products: 63.5 us -> none  [gram_product(): lax.dot_general(left_panel, right_panel, (((0,), (0,)), ((), ())), precis...]
    all_to_all x2 -> x0, blocking collectives: 49.8 us -> none  [the longest x1 27.9 us: per_device(): lax.all_to_all(scaled, 'row', split_axis=1, concat_axis=0, tiled=True)]
    pallas_call x0 -> x9, Pallas kernels: none -> 45.3 us  [kernel_call(): pl.pallas_call(body, out_shape=outs, in_specs=in_specs or [VMEM] * len(ar...]
    gather x1 -> x0, local copies, waits for them, and re-layouts: 11.8 us -> none  [smoothing_tile(): row_degree = jnp.take(degree_cells, row_cell)]
    reshape x3 -> x0, local copies, waits for them, and re-layouts: 8.44 us -> none  [the longest x1 8.3 us: per_device(): right_factor.reshape(row_count, col_count, local_rows, tile_width)]
  transfers between devices with their start and end apart: 2 -> 37, of which waited for: 2 -> 11; matrix products, arithmetic and copies ran while one was open for 9% -> 0% of each run, Pallas kernels for 0% -> 19%
where the time goes in v1:
time: 193 us
  starting transfers between devices  73.1 us (38%)
  waiting for transfers between devices  69.5 us (36%)
  Pallas kernels  45.3 us (23%)
  local copies, waits for them, and re-layouts  4.79 us (2%)
    ppermute x37, starting transfers between devices, send(): return lax.ppermute(block, AXES, pairs)  73.1 us
    ppermute x37, waiting for transfers between devices, send(): return lax.ppermute(block, AXES, pairs)  69.5 us
    pallas_call x9, Pallas kernels, kernel_call(): pl.pallas_call(body, out_shape=outs, in_specs=in_specs or [VMEM] * len(ar...  45.3 us
    unnamed x12, local copies, waits for them, and re-layouts  4.71 us
  transfers between devices with their start and end apart: 37, of which 11 were waited for; matrix products, arithmetic and copies ran while one was open for 0% of the time, Pallas kernels for 19%

profile of v1, /device:TPU:1, one launch (start us, length us, event | category | flops | bytes accessed | tf_op | source)
XLA Modules:
  0.0 192.9 jit_solution(7134673249549558123)
XLA Ops:
  4.1 2.5 %collective-permute-start = (f32[16,2048]{1,0:T(8,128)S(1)}, f32[16,2048]{1,0:T(8,128)S(1)}, u32[]{:S(2)}, u32[]{:S(2)}) collective-permute-start(f32[16,2048]{1,0:T(8,128)S(1)} %get-tuple-element.26), channel_id=1, source_target_pairs={{0,32},{1,33},{2,34},{3,35},{4,36},{5,37},{6,38},{7,39},{8,40},{9,... | collective-permute-start | bytes 393224 | tf_op jit(solution)/shard_map/ppermute | solution.py:36
  6.6 3.3 %collective-permute-start.1 = (f32[16,2048]{1,0:T(8,128)S(1)}, f32[16,2048]{1,0:T(8,128)S(1)}, u32[]{:S(2)}, u32[]{:S(2)}) collective-permute-start(f32[16,2048]{1,0:T(8,128)S(1)} %get-tuple-element.27), channel_id=1, source_target_pairs={{0,64},{1,65},{2,66},{3,67},{4,68},{5,69},{6,70},{7,71},{8,72},{9,... | collective-permute-start | bytes 393224 | tf_op jit(solution)/shard_map/ppermute | solution.py:36
  10.6 2.7 %collective-permute-start.3 = (f32[16,2048]{1,0:T(8,128)S(1)}, f32[16,2048]{1,0:T(8,128)S(1)}, u32[]{:S(2)}, u32[]{:S(2)}) collective-permute-start(f32[16,2048]{1,0:T(8,128)S(1)} %get-tuple-element.29), channel_id=1, source_target_pairs={{0,24},{1,25},{2,26},{3,27},{4,28},{5,29},{6,30},{7,31},{8,16},{9,... | collective-permute-start | bytes 393224 | tf_op jit(solution)/shard_map/ppermute | solution.py:36
  13.8 2.8 %collective-permute-start.5 = (f32[16,2048]{1,0:T(8,128)S(1)}, f32[16,2048]{1,0:T(8,128)S(1)}, u32[]{:S(2)}, u32[]{:S(2)}) collective-permute-start(f32[16,2048]{1,0:T(8,128)S(1)} %get-tuple-element.31), channel_id=1, source_target_pairs={{0,88},{1,89},{2,90},{3,91},{4,92},{5,93},{6,94},{7,95},{8,80},{9,... | collective-permute-start | bytes 393224 | tf_op jit(solution)/shard_map/ppermute | solution.py:36
  25.1 2.5 %collective-permute-start.27 = (f32[128,2048]{1,0:T(8,128)S(1)}, f32[128,2048]{1,0:T(8,128)S(1)}, u32[]{:S(2)}, u32[]{:S(2)}) collective-permute-start(f32[128,2048]{1,0:T(8,128)S(1)} %shard_map.65.refs_0_), channel_id=1, source_target_pairs={{0,2},{1,7},{2,4},{3,1},{4,6},{5,3},{6,0},{7,5},{8,10},{9,15},{10,... | collective-permute-start | bytes 3145736 | tf_op jit(solution)/shard_map/ppermute | solution.py:36
  27.6 2.9 %collective-permute-start.30 = (f32[128,2048]{1,0:T(8,128)S(1)}, f32[128,2048]{1,0:T(8,128)S(1)}, u32[]{:S(2)}, u32[]{:S(2)}) collective-permute-start(f32[128,2048]{1,0:T(8,128)S(1)} %shard_map.65.refs_0_), channel_id=1, source_target_pairs={{0,1},{1,0},{2,3},{3,2},{4,5},{5,4},{6,7},{7,6},{8,9},{9,8},{10,11... | collective-permute-start | bytes 3145736 | tf_op jit(solution)/shard_map/ppermute | solution.py:36
  30.7 2.4 %collective-permute-start.17 = (f32[2,16,1024]{2,1,0:T(8,128)S(1)}, f32[2,16,1024]{2,1,0:T(8,128)S(1)}, u32[]{:S(2)}, u32[]{:S(2)}) collective-permute-start(f32[2,16,1024]{2,1,0:T(8,128)S(1)} %get-tuple-element.37), channel_id=1, source_target_pairs={{0,4},{1,5},{2,6},{3,7},{4,0},{5,1},{6,2},{7,3},{8,12},{9,13},{10,... | collective-permute-start | bytes 393224 | tf_op jit(solution)/shard_map/ppermute | solution.py:36
  33.1 26.4 %collective-permute-done.16.refs_1_ = f32[2,16,1024]{2,1,0:T(8,128)S(1)} collective-permute-done((f32[2,16,1024]{2,1,0:T(8,128)S(1)}, f32[2,16,1024]{2,1,0:T(8,128)S(1)}, u32[]{:S(2)}, u32[]{:S(2)}) %collective-permute-start.16) | collective-permute-done | bytes 131104 | tf_op jit(solution)/shard_map/ppermute | solution.py:36
  65.6 3.3 %collective-permute-start.21 = (f32[2,16,1024]{2,1,0:T(8,128)S(1)}, f32[2,16,1024]{2,1,0:T(8,128)S(1)}, u32[]{:S(2)}, u32[]{:S(2)}) collective-permute-start(f32[2,16,1024]{2,1,0:T(8,128)S(1)} %get-tuple-element.41), channel_id=1, source_target_pairs={{0,28},{1,29},{2,30},{3,31},{4,24},{5,25},{6,26},{7,27},{8,20},{9,... | collective-permute-start | bytes 393224 | tf_op jit(solution)/shard_map/ppermute | solution.py:36
  71.2 2.5 %collective-permute-start.22 = (f32[2,16,1024]{2,1,0:T(8,128)S(1)}, f32[2,16,1024]{2,1,0:T(8,128)S(1)}, u32[]{:S(2)}, u32[]{:S(2)}) collective-permute-start(f32[2,16,1024]{2,1,0:T(8,128)S(1)} %get-tuple-element.42), channel_id=1, source_target_pairs={{0,30},{1,31},{2,24},{3,25},{4,26},{5,27},{6,28},{7,29},{8,22},{9,... | collective-permute-start | bytes 393224 | tf_op jit(solution)/shard_map/ppermute | solution.py:36
  74.7 2.7 %collective-permute-done.22.refs_7_ = f32[2,16,1024]{2,1,0:T(8,128)S(1)} collective-permute-done((f32[2,16,1024]{2,1,0:T(8,128)S(1)}, f32[2,16,1024]{2,1,0:T(8,128)S(1)}, u32[]{:S(2)}, u32[]{:S(2)}) %collective-permute-start.22) | collective-permute-done | bytes 131104 | tf_op jit(solution)/shard_map/ppermute | solution.py:36
  81.5 14.5 %collective-permute-done.7.refs_0_ = f32[128,2048]{1,0:T(8,128)S(1)} collective-permute-done((f32[128,2048]{1,0:T(8,128)S(1)}, f32[128,2048]{1,0:T(8,128)S(1)}, u32[]{:S(2)}, u32[]{:S(2)}) %collective-permute-start.7) | collective-permute-done | bytes 1048608 | tf_op jit(solution)/shard_map/ppermute | solution.py:36
  96.1 8.0 %collective-permute-start.31 = (f32[128,2048]{1,0:T(8,128)S(1)}, f32[128,2048]{1,0:T(8,128)S(1)}, u32[]{:S(2)}, u32[]{:S(2)}) collective-permute-start(f32[128,2048]{1,0:T(8,128)S(1)} %collective-permute-done.27.refs_1_), channel_id=1, source_target_pairs={{0,1},{1,0},{2,3},{3,2},{4,5},{5,4},{6,7},{7,6},{8,9},{9,8},{10,11... | collective-permute-start | bytes 3145736 | tf_op jit(solution)/shard_map/ppermute | solution.py:36
  107.8 14.1 %collective-permute-done.23.refs_8_ = f32[256,1024]{1,0:T(8,128)S(1)} collective-permute-done((f32[256,1024]{1,0:T(8,128)S(1)}, f32[256,1024]{1,0:T(8,128)S(1)}, u32[]{:S(2)}, u32[]{:S(2)}) %collective-permute-start.23) | collective-permute-done | bytes 1048608 | tf_op jit(solution)/shard_map/ppermute | solution.py:36
  121.9 2.8 %collective-permute-start.33 = (f32[128,2048]{1,0:T(8,128)S(1)}, f32[128,2048]{1,0:T(8,128)S(1)}, u32[]{:S(2)}, u32[]{:S(2)}) collective-permute-start(f32[128,2048]{1,0:T(8,128)S(1)} %collective-permute-done.29.refs_3_), channel_id=1, source_target_pairs={{0,1},{1,0},{2,3},{3,2},{4,5},{5,4},{6,7},{7,6},{8,9},{9,8},{10,11... | collective-permute-start | bytes 3145736 | tf_op jit(solution)/shard_map/ppermute | solution.py:36
  126.2 5.7 %shard_map.68 = (f32[8,2048]{1,0:T(8,128)S(1)}, f32[8,1024]{1,0:T(8,128)S(1)}) custom-call(s32[8]{0:T(128)S(1)} %stack.39.spot, s32[1,8192]{1,0:T(1,128)S(1)} %bitcast.14, f32[1,8192]{1,0:T(1,128)S(1)} %bitcast.15), custom_call_target="tpu_custom_call" | custom-call | flops 1073741824 | bytes 1048576 | tf_op jit(solution)/shard_map/pallas_call | solution.py:40
  132.7 2.9 %collective-permute-start.24 = (f32[256,1024]{1,0:T(8,128)S(1)}, f32[256,1024]{1,0:T(8,128)S(1)}, u32[]{:S(2)}, u32[]{:S(2)}) collective-permute-start(f32[256,1024]{1,0:T(8,128)S(1)} %collective-permute-done.23.refs_8_), channel_id=1, source_target_pairs={{0,32},{1,97},{2,34},{3,99},{4,36},{5,101},{6,38},{7,103},{8,40},{... | collective-permute-start | bytes 3145736 | tf_op jit(solution)/shard_map/ppermute | solution.py:36
  137.8 9.0 %shard_map.69.refs_14_ = f32[2048,1024]{1,0:T(8,128)S(1)} custom-call(s32[8]{0:T(128)S(1)} %stack.39.spot, f32[128,2048]{1,0:T(8,128)S(1)} %shard_map.65.refs_0_, f32[128,2048]{1,0:T(8,128)S(1)} %collective-permute-done.27.refs_1_, f32[128,2048]{1,0:T(8,128)S(1)} %collective-permute-done.28.refs_2_, f32[128,2048]{1,0:T(8,128)S(1)} %collective-permute-done.29.refs_3_, ...), custom_call_target="tpu_custom_call" | custom-call | flops 12884901888 | bytes 25165824 | tf_op jit(solution)/shard_map/pallas_call | solution.py:40
  148.7 5.9 %collective-permute-start.12 = (f32[128,2048]{1,0:T(8,128)S(1)}, f32[128,2048]{1,0:T(8,128)S(1)}, u32[]{:S(2)}, u32[]{:S(2)}) collective-permute-start(f32[128,2048]{1,0:T(8,128)S(1)} %collective-permute-done.8.refs_1_), channel_id=1, source_target_pairs={{0,1},{1,0},{2,3},{3,2},{4,5},{5,4},{6,7},{7,6},{8,9},{9,8},{10,11... | collective-permute-start | bytes 3145736 | tf_op jit(solution)/shard_map/ppermute | solution.py:36
  154.7 3.3 %collective-permute-start.25 = (f32[256,1024]{1,0:T(8,128)S(1)}, f32[256,1024]{1,0:T(8,128)S(1)}, u32[]{:S(2)}, u32[]{:S(2)}) collective-permute-start(f32[256,1024]{1,0:T(8,128)S(1)} %collective-permute-done.24.refs_9_), channel_id=1, source_target_pairs={{0,32},{1,97},{2,34},{3,99},{4,36},{5,101},{6,38},{7,103},{8,40},{... | collective-permute-start | bytes 3145736 | tf_op jit(solution)/shard_map/ppermute | solution.py:36
  158.0 5.2 %collective-permute-start.14 = (f32[128,2048]{1,0:T(8,128)S(1)}, f32[128,2048]{1,0:T(8,128)S(1)}, u32[]{:S(2)}, u32[]{:S(2)}) collective-permute-start(f32[128,2048]{1,0:T(8,128)S(1)} %collective-permute-done.10.refs_3_), channel_id=1, source_target_pairs={{0,1},{1,0},{2,3},{3,2},{4,5},{5,4},{6,7},{7,6},{8,9},{9,8},{10,11... | collective-permute-start | bytes 3145736 | tf_op jit(solution)/shard_map/ppermute | solution.py:36
  163.2 9.0 %shard_map.70.refs_11_ = f32[2048,1024]{1,0:T(8,128)S(1)} custom-call(s32[8]{0:T(128)S(1)} %stack.39.spot, f32[128,2048]{1,0:T(8,128)S(1)} %shard_map.65.refs_0_, f32[128,2048]{1,0:T(8,128)S(1)} %collective-permute-done.27.refs_1_, f32[128,2048]{1,0:T(8,128)S(1)} %collective-permute-done.28.refs_2_, ...), custom_call_target="tpu_custom_call", output_to_operand_aliasing={{}: (15, {})} | custom-call | flops 12884901888 | bytes 25165824 | tf_op jit(solution)/shard_map/pallas_call | solution.py:40
  172.2 12.8 %shard_map.71.refs_9_ = f32[2048,1024]{1,0:T(8,128)S(1)} custom-call(s32[8]{0:T(128)S(1)} %stack.39.spot, f32[128,2048]{1,0:T(8,128)S(1)} %collective-permute-done.7.refs_0_, f32[128,2048]{1,0:T(8,128)S(1)} %collective-permute-done.8.refs_1_, f32[128,2048]{1,0:T(8,128)S(1)} %collective-permute-done.9.refs_2_, ...), custom_call_target="tpu_custom_call", output_to_operand_aliasing={{}: (12, {})} | custom-call | flops 9663676416 | bytes 25165824 | tf_op jit(solution)/shard_map/pallas_call | solution.py:40
  185.0 7.8 %shard_map.72 = f32[2048,1024]{1,0:T(8,128)} custom-call(s32[8]{0:T(128)S(1)} %stack.39.spot, f32[128,2048]{1,0:T(8,128)S(1)} %collective-permute-done.7.refs_0_, f32[128,2048]{1,0:T(8,128)S(1)} %collective-permute-done.8.refs_1_, f32[128,2048]{1,0:T(8,128)S(1)} %collective-permute-done.9.refs_2_, f32[128,2048]{1,0:T(8,128)S(1)} %collective-permute-done.10.refs_3_, ...), custom_call_target="tpu_custom_call" | custom-call | flops 3221225472 | bytes 25165824 | tf_op jit(solution)/shard_map/pallas_call | solution.py:40
  (72 shorter events, 37.3 us)
Async XLA Ops:
  25.1 53.5 %collective-permute-start.27 = (f32[128,2048]{1,0:T(8,128)S(1)}, f32[128,2048]{1,0:T(8,128)S(1)}, u32[]{:S(2)}, u32[]{:S(2)}) collective-permute-start(f32[128,2048]{1,0:T(8,128)S(1)} %shard_map.65.refs_0_), channel_id=1, source_target_pairs={{0,2},{1,7},{2,4},{3,1},{4,6},{5,3},{6,0},{7,5},{8,10},{9,15},{10,... | collective-permute-start | bytes 3145736 | tf_op jit(solution)/shard_map/ppermute | solution.py:36
  27.6 51.4 %collective-permute-start.28 = (f32[128,2048]{1,0:T(8,128)S(1)}, f32[128,2048]{1,0:T(8,128)S(1)}, u32[]{:S(2)}, u32[]{:S(2)}) collective-permute-start(f32[128,2048]{1,0:T(8,128)S(1)} %shard_map.65.refs_0_), channel_id=1, source_target_pairs={{0,6},{1,3},{2,0},{3,5},{4,2},{5,7},{6,4},{7,1},{8,14},{9,11},{10,... | collective-permute-start | bytes 3145736 | tf_op jit(solution)/shard_map/ppermute | solution.py:36
  27.6 52.1 %collective-permute-start.30 = (f32[128,2048]{1,0:T(8,128)S(1)}, f32[128,2048]{1,0:T(8,128)S(1)}, u32[]{:S(2)}, u32[]{:S(2)}) collective-permute-start(f32[128,2048]{1,0:T(8,128)S(1)} %shard_map.65.refs_0_), channel_id=1, source_target_pairs={{0,1},{1,0},{2,3},{3,2},{4,5},{5,4},{6,7},{7,6},{8,9},{9,8},{10,11... | collective-permute-start | bytes 3145736 | tf_op jit(solution)/shard_map/ppermute | solution.py:36
  30.6 28.9 %collective-permute-start.16 = (f32[2,16,1024]{2,1,0:T(8,128)S(1)}, f32[2,16,1024]{2,1,0:T(8,128)S(1)}, u32[]{:S(2)}, u32[]{:S(2)}) collective-permute-start(f32[2,16,1024]{2,1,0:T(8,128)S(1)} %get-tuple-element.36), channel_id=1, source_target_pairs={{0,2},{1,3},{2,4},{3,5},{4,6},{5,7},{6,0},{7,1},{8,10},{9,11},{10,... | collective-permute-start | bytes 393224 | tf_op jit(solution)/shard_map/ppermute | solution.py:36
  30.7 28.8 %collective-permute-start.17 = (f32[2,16,1024]{2,1,0:T(8,128)S(1)}, f32[2,16,1024]{2,1,0:T(8,128)S(1)}, u32[]{:S(2)}, u32[]{:S(2)}) collective-permute-start(f32[2,16,1024]{2,1,0:T(8,128)S(1)} %get-tuple-element.37), channel_id=1, source_target_pairs={{0,4},{1,5},{2,6},{3,7},{4,0},{5,1},{6,2},{7,3},{8,12},{9,13},{10,... | collective-permute-start | bytes 393224 | tf_op jit(solution)/shard_map/ppermute | solution.py:36
  74.7 21.4 %collective-permute-start.7 = (f32[128,2048]{1,0:T(8,128)S(1)}, f32[128,2048]{1,0:T(8,128)S(1)}, u32[]{:S(2)}, u32[]{:S(2)}) collective-permute-start(f32[128,2048]{1,0:T(8,128)S(1)} %shard_map.65.refs_0_), channel_id=1, source_target_pairs={{0,8},{1,9},{2,10},{3,11},{4,12},{5,13},{6,14},{7,15},{8,0},{9,1},... | collective-permute-start | bytes 3145736 | tf_op jit(solution)/shard_map/ppermute | solution.py:36
  77.5 26.6 %collective-permute-start.34 = (f32[256,1024]{1,0:T(8,128)S(1)}, f32[256,1024]{1,0:T(8,128)S(1)}, u32[]{:S(2)}, u32[]{:S(2)}) collective-permute-start(f32[256,1024]{1,0:T(8,128)S(1)} %shard_map.67.refs_8_), channel_id=1, source_target_pairs={{0,32},{1,97},{2,34},{3,99},{4,36},{5,101},{6,38},{7,103},{8,40},{... | collective-permute-start | bytes 3145736 | tf_op jit(solution)/shard_map/ppermute | solution.py:36
  78.6 26.8 %collective-permute-start.35 = (f32[256,1024]{1,0:T(8,128)S(1)}, f32[256,1024]{1,0:T(8,128)S(1)}, u32[]{:S(2)}, u32[]{:S(2)}) collective-permute-start(f32[256,1024]{1,0:T(8,128)S(1)} %shard_map.67.refs_8_), channel_id=1, source_target_pairs={{0,96},{1,33},{2,98},{3,35},{4,100},{5,37},{6,102},{7,39},{8,104},... | collective-permute-start | bytes 3145736 | tf_op jit(solution)/shard_map/ppermute | solution.py:36
  79.0 42.9 %collective-permute-start.23 = (f32[256,1024]{1,0:T(8,128)S(1)}, f32[256,1024]{1,0:T(8,128)S(1)}, u32[]{:S(2)}, u32[]{:S(2)}) collective-permute-start(f32[256,1024]{1,0:T(8,128)S(1)} %shard_map.67.refs_8_), channel_id=1, source_target_pairs={{0,16},{1,17},{2,18},{3,19},{4,20},{5,21},{6,22},{7,23},{8,24},{9,... | collective-permute-start | bytes 3145736 | tf_op jit(solution)/shard_map/ppermute | solution.py:36
  79.7 42.2 %collective-permute-start.29 = (f32[128,2048]{1,0:T(8,128)S(1)}, f32[128,2048]{1,0:T(8,128)S(1)}, u32[]{:S(2)}, u32[]{:S(2)}) collective-permute-start(f32[128,2048]{1,0:T(8,128)S(1)} %collective-permute-done.27.refs_1_), channel_id=1, source_target_pairs={{0,2},{1,7},{2,4},{3,1},{4,6},{5,3},{6,0},{7,5},{8,10},{9,15},{10,... | collective-permute-start | bytes 3145736 | tf_op jit(solution)/shard_map/ppermute | solution.py:36
  96.1 35.9 %collective-permute-start.31 = (f32[128,2048]{1,0:T(8,128)S(1)}, f32[128,2048]{1,0:T(8,128)S(1)}, u32[]{:S(2)}, u32[]{:S(2)}) collective-permute-start(f32[128,2048]{1,0:T(8,128)S(1)} %collective-permute-done.27.refs_1_), channel_id=1, source_target_pairs={{0,1},{1,0},{2,3},{3,2},{4,5},{5,4},{6,7},{7,6},{8,9},{9,8},{10,11... | collective-permute-start | bytes 3145736 | tf_op jit(solution)/shard_map/ppermute | solution.py:36
  104.1 27.9 %collective-permute-start.32 = (f32[128,2048]{1,0:T(8,128)S(1)}, f32[128,2048]{1,0:T(8,128)S(1)}, u32[]{:S(2)}, u32[]{:S(2)}) collective-permute-start(f32[128,2048]{1,0:T(8,128)S(1)} %collective-permute-done.28.refs_2_), channel_id=1, source_target_pairs={{0,1},{1,0},{2,3},{3,2},{4,5},{5,4},{6,7},{7,6},{8,9},{9,8},{10,11... | collective-permute-start | bytes 3145736 | tf_op jit(solution)/shard_map/ppermute | solution.py:36
  105.4 27.2 %collective-permute-start.8 = (f32[128,2048]{1,0:T(8,128)S(1)}, f32[128,2048]{1,0:T(8,128)S(1)}, u32[]{:S(2)}, u32[]{:S(2)}) collective-permute-start(f32[128,2048]{1,0:T(8,128)S(1)} %collective-permute-done.7.refs_0_), channel_id=1, source_target_pairs={{0,2},{1,7},{2,4},{3,1},{4,6},{5,3},{6,0},{7,5},{8,10},{9,15},{10,... | collective-permute-start | bytes 3145736 | tf_op jit(solution)/shard_map/ppermute | solution.py:36
  121.9 13.9 %collective-permute-start.36 = (f32[256,1024]{1,0:T(8,128)S(1)}, f32[256,1024]{1,0:T(8,128)S(1)}, u32[]{:S(2)}, u32[]{:S(2)}) collective-permute-start(f32[256,1024]{1,0:T(8,128)S(1)} %collective-permute-done.34.refs_9_), channel_id=1, source_target_pairs={{0,32},{1,97},{2,34},{3,99},{4,36},{5,101},{6,38},{7,103},{8,40},{... | collective-permute-start | bytes 3145736 | tf_op jit(solution)/shard_map/ppermute | solution.py:36
  121.9 13.9 %collective-permute-start.33 = (f32[128,2048]{1,0:T(8,128)S(1)}, f32[128,2048]{1,0:T(8,128)S(1)}, u32[]{:S(2)}, u32[]{:S(2)}) collective-permute-start(f32[128,2048]{1,0:T(8,128)S(1)} %collective-permute-done.29.refs_3_), channel_id=1, source_target_pairs={{0,1},{1,0},{2,3},{3,2},{4,5},{5,4},{6,7},{7,6},{8,9},{9,8},{10,11... | collective-permute-start | bytes 3145736 | tf_op jit(solution)/shard_map/ppermute | solution.py:36
  131.9 16.8 %collective-permute-start.9 = (f32[128,2048]{1,0:T(8,128)S(1)}, f32[128,2048]{1,0:T(8,128)S(1)}, u32[]{:S(2)}, u32[]{:S(2)}) collective-permute-start(f32[128,2048]{1,0:T(8,128)S(1)} %collective-permute-done.7.refs_0_), channel_id=1, source_target_pairs={{0,6},{1,3},{2,0},{3,5},{4,2},{5,7},{6,4},{7,1},{8,14},{9,11},{10,... | collective-permute-start | bytes 3145736 | tf_op jit(solution)/shard_map/ppermute | solution.py:36
  132.0 22.6 %collective-permute-start.11 = (f32[128,2048]{1,0:T(8,128)S(1)}, f32[128,2048]{1,0:T(8,128)S(1)}, u32[]{:S(2)}, u32[]{:S(2)}) collective-permute-start(f32[128,2048]{1,0:T(8,128)S(1)} %collective-permute-done.7.refs_0_), channel_id=1, source_target_pairs={{0,1},{1,0},{2,3},{3,2},{4,5},{5,4},{6,7},{7,6},{8,9},{9,8},{10,11... | collective-permute-start | bytes 3145736 | tf_op jit(solution)/shard_map/ppermute | solution.py:36
  132.7 22.0 %collective-permute-start.24 = (f32[256,1024]{1,0:T(8,128)S(1)}, f32[256,1024]{1,0:T(8,128)S(1)}, u32[]{:S(2)}, u32[]{:S(2)}) collective-permute-start(f32[256,1024]{1,0:T(8,128)S(1)} %collective-permute-done.23.refs_8_), channel_id=1, source_target_pairs={{0,32},{1,97},{2,34},{3,99},{4,36},{5,101},{6,38},{7,103},{8,40},{... | collective-permute-start | bytes 3145736 | tf_op jit(solution)/shard_map/ppermute | solution.py:36
  135.9 36.3 %collective-permute-start.26 = (f32[256,1024]{1,0:T(8,128)S(1)}, f32[256,1024]{1,0:T(8,128)S(1)}, u32[]{:S(2)}, u32[]{:S(2)}) collective-permute-start(f32[256,1024]{1,0:T(8,128)S(1)} %collective-permute-done.23.refs_8_), channel_id=1, source_target_pairs={{0,96},{1,33},{2,98},{3,35},{4,100},{5,37},{6,102},{7,39},{8,104},... | collective-permute-start | bytes 3145736 | tf_op jit(solution)/shard_map/ppermute | solution.py:36
  135.9 22.1 %collective-permute-start.10 = (f32[128,2048]{1,0:T(8,128)S(1)}, f32[128,2048]{1,0:T(8,128)S(1)}, u32[]{:S(2)}, u32[]{:S(2)}) collective-permute-start(f32[128,2048]{1,0:T(8,128)S(1)} %collective-permute-done.8.refs_1_), channel_id=1, source_target_pairs={{0,2},{1,7},{2,4},{3,1},{4,6},{5,3},{6,0},{7,5},{8,10},{9,15},{10,... | collective-permute-start | bytes 3145736 | tf_op jit(solution)/shard_map/ppermute | solution.py:36
  148.7 23.5 %collective-permute-start.12 = (f32[128,2048]{1,0:T(8,128)S(1)}, f32[128,2048]{1,0:T(8,128)S(1)}, u32[]{:S(2)}, u32[]{:S(2)}) collective-permute-start(f32[128,2048]{1,0:T(8,128)S(1)} %collective-permute-done.8.refs_1_), channel_id=1, source_target_pairs={{0,1},{1,0},{2,3},{3,2},{4,5},{5,4},{6,7},{7,6},{8,9},{9,8},{10,11... | collective-permute-start | bytes 3145736 | tf_op jit(solution)/shard_map/ppermute | solution.py:36
  154.7 17.5 %collective-permute-start.13 = (f32[128,2048]{1,0:T(8,128)S(1)}, f32[128,2048]{1,0:T(8,128)S(1)}, u32[]{:S(2)}, u32[]{:S(2)}) collective-permute-start(f32[128,2048]{1,0:T(8,128)S(1)} %collective-permute-done.9.refs_2_), channel_id=1, source_target_pairs={{0,1},{1,0},{2,3},{3,2},{4,5},{5,4},{6,7},{7,6},{8,9},{9,8},{10,11... | collective-permute-start | bytes 3145736 | tf_op jit(solution)/shard_map/ppermute | solution.py:36
  154.7 30.3 %collective-permute-start.25 = (f32[256,1024]{1,0:T(8,128)S(1)}, f32[256,1024]{1,0:T(8,128)S(1)}, u32[]{:S(2)}, u32[]{:S(2)}) collective-permute-start(f32[256,1024]{1,0:T(8,128)S(1)} %collective-permute-done.24.refs_9_), channel_id=1, source_target_pairs={{0,32},{1,97},{2,34},{3,99},{4,36},{5,101},{6,38},{7,103},{8,40},{... | collective-permute-start | bytes 3145736 | tf_op jit(solution)/shard_map/ppermute | solution.py:36
  158.0 14.2 %collective-permute-start.14 = (f32[128,2048]{1,0:T(8,128)S(1)}, f32[128,2048]{1,0:T(8,128)S(1)}, u32[]{:S(2)}, u32[]{:S(2)}) collective-permute-start(f32[128,2048]{1,0:T(8,128)S(1)} %collective-permute-done.10.refs_3_), channel_id=1, source_target_pairs={{0,1},{1,0},{2,3},{3,2},{4,5},{5,4},{6,7},{7,6},{8,9},{9,8},{10,11... | collective-permute-start | bytes 3145736 | tf_op jit(solution)/shard_map/ppermute | solution.py:36
  (19 other events, 113.5 us)

commit v2 on v1

--- a/solution.py
+++ b/solution.py
@@ -54,16 +54,17 @@
 
 VMEM = pl.BlockSpec(memory_space=pltpu.VMEM)
 SMEM = pl.BlockSpec(memory_space=pltpu.SMEM)
-
-
-def scale_body(spot, scales, green, noise, sets, *outs):
+HBM = pl.BlockSpec(memory_space=pltpu.HBM)
+
+
+def scale_body(spot, green, pack, *outs):
     row_pieces, mine, theirs = outs[:8], outs[8], outs[9]
     z, y_hi, y_lo, x, core = (spot[i] for i in range(5))
-    chosen = sets[...]
-    factor = jnp.zeros_like(noise[...])
+    noise, chosen = pack[0:1, 0:16], pack[0:1, 16:32]
+    factor = jnp.zeros_like(noise)
     for s in range(4):
-        factor = jnp.where(chosen == s, scales[s], factor)
-    root = jnp.broadcast_to(jnp.sqrt(noise[...] * factor), (16, 16))
+        factor = jnp.where(chosen == float(s), pack[0:1, 32 + s : 33 + s], factor)
+    root = jnp.broadcast_to(jnp.sqrt(noise * factor), (16, 16))
     eye = lax.broadcasted_iota(jnp.int32, (16, 16), 0) == lax.broadcasted_iota(jnp.int32, (16, 16), 1)
     root = jnp.sum(jnp.where(eye, root, 0.0), axis=1, keepdims=True)
     for c in range(2):
@@ -156,25 +157,45 @@
     return jnp.where(spacing == 0.0, sides[:, 3:4], coupling)
 
 
-def split_right(late, core, right, spots, high, low):
-    depth = 32 * len(right)
-    for n in range(4):
-        for j in range(2):
-            who = core if j == 0 else 1 - core
-            dx = (0, 1 + 2 * who, 3 - 2 * who, 2)[n]
-            for ref, at in zip(right, spots):
-                for c in range(2):
-                    c_from = 1 - c if late else c
-                    source = pl.multiple_of(dx * 64 + c_from * 32 + j * 16, 16)
-                    target = pl.multiple_of((j * 4 + n) * depth + at * 32 + c * 16, 16)
-                    piece = ref[pl.ds(source, 16), :]
-                    top = piece.astype(jnp.bfloat16)
-                    high[pl.ds(target, 16), :] = top
-                    low[pl.ds(target, 16), :] = (piece - top.astype(jnp.float32)).astype(jnp.bfloat16)
-
-
-def product(left, rows, part, high, low):
-    block = jnp.concatenate([ref[a:b, part] for ref in left for a, b in rows], 0).T
+EARLY = ((0, 1, 3), (0, 1, 3), (0, 1, 3), (), (0, 1, 3), (1, 3), (1, 3), ())
+REST = ((2,), (2,), (2,), (0, 1, 2, 3), (2,), (0, 2), (0, 2), (0, 1, 2, 3))
+TILE = 256
+
+
+def split_right(late, plan, core, right, high, low):
+    start = 0
+    for i, chosen in enumerate(plan):
+        who = core if i < 4 else 1 - core
+        dx = (0, 1 + 2 * who, 3 - 2 * who, 2)[i % 4]
+        at = {dz: start + 32 * k for k, dz in enumerate(chosen)}
+        targets = []
+        if 0 in at:
+            targets.append((0, at[0]))
+        if 1 in at:
+            targets.append((1, at[1] + core * (at[3] - at[1])))
+            targets.append((2, at[3] + core * (at[1] - at[3])))
+        if 2 in at:
+            targets.append((3, at[2]))
+        for m, base in targets:
+            for c in range(2):
+                c_from = 1 - c if late else c
+                source = pl.multiple_of(dx * 64 + c_from * 32 + i // 4 * 16, 16)
+                target = pl.multiple_of(base + c * 16, 16)
+                piece = right[m][pl.ds(source, 16), :]
+                top = piece.astype(jnp.bfloat16)
+                high[pl.ds(target, 16), :] = top
+                low[pl.ds(target, 16), :] = (piece - top.astype(jnp.float32)).astype(jnp.bfloat16)
+        start += 32 * len(chosen)
+
+
+def product(left, plan, part, high, low):
+    refs = iter(left)
+    rows = []
+    for chosen in plan:
+        if chosen:
+            ref = next(refs)
+            rows += [ref[dz * 32 : dz * 32 + 32, part] for dz in chosen]
+    block = jnp.concatenate(rows, 0).T
     top = block.astype(jnp.bfloat16)
     rest = (block - top.astype(jnp.float32)).astype(jnp.bfloat16)
 
@@ -184,67 +205,65 @@
     return dot(top, high[...]) + (dot(top, low[...]) + dot(rest, high[...]))
 
 
-ALL = ((0, 128),)
-MOST = ((0, 64), (96, 128))
-FAR = ((64, 96),)
-
-
-def near_body(start, stop, spot, *refs):
-    left, right = refs[:8], refs[8:12]
-    row_side, col_side = refs[12:14]
-    out, high, low = refs[-3:]
-    core = spot[4]
-    split_right(False, core, right, (0, 1 + 2 * core, 3 - 2 * core, 2), high, low)
-
-    @pl.loop(start // TILE, stop // TILE)
+def gram_body(plan, late, last, spot, *refs):
+    n_left = sum(1 for chosen in plan if chosen)
+    n_right = 3 if plan is EARLY else 4
+    left, right = refs[:n_left], refs[n_left : n_left + n_right]
+    if last:
+        *extra, result, high, low, out, sent = refs[n_left + n_right :]
+    else:
+        *extra, out, high, low = refs[n_left + n_right :]
+    split_right(late, plan, spot[4], right, high, low)
+
+    def copy(i):
+        part = pl.ds(pl.multiple_of(i * TILE, TILE), TILE)
+        return pltpu.make_async_copy(out.at[part, :], result.at[part, :], sent.at[i])
+
+    @pl.loop(0, ROWS // TILE, unroll=UNROLL)
     def _(i):
         part = pl.ds(pl.multiple_of(i * TILE, TILE), TILE)
-        out[part, :] = product(left, ALL, part, high, low) + prior_tile(spot, row_side[:, part], col_side)
-
-
-def late_body(spot, *refs):
-    left, right = refs[:8], refs[8:11]
-    total, out, high, low = refs[11:]
-    core = spot[4]
-    split_right(True, core, right, (0, 1 + core, 2 - core), high, low)
-
-    @pl.loop(0, ROWS // TILE)
-    def _(i):
-        part = pl.ds(pl.multiple_of(i * TILE, TILE), TILE)
-        out[part, :] = total[part, :] + product(left, MOST, part, high, low)
-
-
-def far_body(spot, *refs):
-    left, right = refs[:8], refs[8:9]
-    total, out, high, low = refs[9:]
-
-    @pl.when(pl.program_id(0) == 0)
-    def _():
-        split_right(True, spot[4], right, (0,), high, low)
-
-    part = pl.ds(pl.multiple_of(pl.program_id(0) * TILE, TILE), TILE)
-    out[...] = total[part, :] + product(left, FAR, part, high, low)
-
-
-TILE = 256
-
-
-def gram_call(body, depth, spot, *args, **extra):
-    args = (spot, *args)
+        block = product(left, plan, part, high, low)
+        if len(extra) == 1:
+            out[part, :] = extra[0][part, :] + block
+        else:
+            out[part, :] = block + prior_tile(spot, extra[0][:, part], extra[1])
+        if last:
+            copy(i).start()
+
+    if last:
+        for i in range(ROWS // TILE):
+            copy(i).wait()
+
+
+UNROLL = 4
+
+
+def gram_call(plan, late, last, spot, left, right, extra):
+    left = [ref for ref, chosen in zip(left, plan) if chosen]
+    right = right[:3] if plan is EARLY else right
+    depth = 32 * sum(len(chosen) for chosen in plan)
+    args = (spot, *left, *right, *extra)
+    options = {}
+    scratch = [pltpu.VMEM((depth, COLS), jnp.bfloat16)] * 2
+    if last:
+        options = dict(out_specs=HBM)
+        scratch += [pltpu.VMEM((ROWS, COLS), jnp.float32), pltpu.SemaphoreType.DMA((ROWS // TILE,))]
+    elif len(extra) == 1:
+        options = dict(input_output_aliases={len(args) - 1: 0})
     return kernel_call(
-        body,
+        functools.partial(gram_body, plan, late, last),
         shape(ROWS, COLS),
         args,
         in_specs=[SMEM] + [VMEM] * (len(args) - 1),
-        scratch=[pltpu.VMEM((depth, COLS), jnp.bfloat16)] * 2,
+        scratch=scratch,
         flops=3 * 2 * ROWS * COLS * depth,
         nbytes=24 << 20,
-        limit=12,
-        **extra,
+        limit=20 if last else 12,
+        **options,
     )
 
 
-def ring(block, axis):
+def ring(block, axis, across=None):
     def shift(sign):
         def target(z, y, x, core):
             step = sign if core == 0 else -sign
@@ -254,7 +273,10 @@
 
     first = send(block, shift(1))
     second = send(block, shift(-1))
-    far = send(first, shift(1))
+    if across is None:
+        far = send(first, shift(1))
+    else:
+        far = send(across, lambda z, y, x, core: (z, DIAGONAL[y], x, core))
     return [block, first, second, far]
 
 
@@ -293,11 +315,12 @@
             (row_start // PATCHES == col_start // PATCHES).astype(jnp.int32),
         ]
     ).astype(jnp.int32)
+    pack = jnp.concatenate([noise_precision, data_set.astype(jnp.float32), set_scale, jnp.zeros((92,), jnp.float32)])
     *row_pieces, mine, theirs = kernel_call(
         scale_body,
         [shape(16, 2048)] * 8 + [shape(8, 16, 1024)] * 2,
-        (spot, set_scale, green, noise_precision.reshape(1, 16), data_set.reshape(1, 16)),
-        in_specs=[SMEM, SMEM, VMEM, VMEM, VMEM],
+        (spot, green, pack.reshape(1, -1)),
+        in_specs=[SMEM, VMEM, VMEM],
         flops=1 << 20,
         nbytes=3 << 20,
     )
@@ -320,31 +343,13 @@
     row_near = ring(row_near, "x")
     col_near = ring(col_near, "z")
     row_late = ring(row_late, "x")
-    col_late = ring(col_late, "z")
+    col_late = ring(col_late, "z", col_near[3])
     left = row_near + swap(row_near)
-    total = gram_call(functools.partial(near_body, 0, ROWS // 2), 1024, spot, *left, *col_near, *sides)
-    total = gram_call(
-        functools.partial(near_body, ROWS // 2, ROWS),
-        1024,
-        spot,
-        *left,
-        *col_near,
-        *sides,
-        total,
-        input_output_aliases={15: 0},
-    )
+    total = gram_call(EARLY, False, False, spot, left, col_near, sides)
+    total = gram_call(REST, False, False, spot, left, col_near, [total])
     left = row_late + swap(row_late)
-    total = gram_call(late_body, 768, spot, *left, *col_late[:3], total, input_output_aliases={12: 0})
-    return gram_call(
-        far_body,
-        256,
-        spot,
-        *left,
-        col_late[3],
-        total,
-        grid=(ROWS // TILE,),
-        out_specs=pl.BlockSpec((TILE, COLS), lambda i: (i, 0)),
-    )
+    total = gram_call(EARLY, True, False, spot, left, col_late, [total])
+    return gram_call(REST, True, True, spot, left, col_late, [total])
 
 
 def solution(mesh):

time: 193 us -> 199 us (1.031)
  waiting for transfers between devices: 69.5 us -> 92.4 us
  starting transfers between devices: 73.1 us -> 58.6 us
  Pallas kernels: 45.3 us -> 41.7 us
    ppermute x37, waiting for transfers between devices: 69.5 us -> 92.4 us  [send(): return lax.ppermute(block, AXES, pairs)]
    ppermute x37, starting transfers between devices: 73.1 us -> 58.6 us  [send(): return lax.ppermute(block, AXES, pairs)]
    pallas_call x9, Pallas kernels: 45.3 us -> 41.7 us  [kernel_call(): pl.pallas_call(body, out_shape=outs, in_specs=in_specs or [VMEM] * len(ar...]
    unnamed x12 -> x6, local copies, waits for them, and re-layouts: 4.71 us -> 2.74 us
  transfers between devices with their start and end apart: 37 -> 37, of which waited for: 11 -> 11; matrix products, arithmetic and copies ran while one was open for 0% -> 0% of each run, Pallas kernels for 19% -> 16%
where the time goes in v2:
time: 199 us; the launch traced here: 197 us
  waiting for transfers between devices  92.4 us (46%)
  starting transfers between devices  58.6 us (29%)
  Pallas kernels  41.7 us (21%)
  local copies, waits for them, and re-layouts  2.83 us (1%)
    ppermute x37, waiting for transfers between devices, send(): return lax.ppermute(block, AXES, pairs)  92.4 us
    ppermute x37, starting transfers between devices, send(): return lax.ppermute(block, AXES, pairs)  58.6 us
    pallas_call x9, Pallas kernels, kernel_call(): pl.pallas_call(body, out_shape=outs, in_specs=in_specs or [VMEM] * len(ar...  41.7 us
  transfers between devices with their start and end apart: 37, of which 11 were waited for; matrix products, arithmetic and copies ran while one was open for 0% of the time, Pallas kernels for 16%

profile of v2, /device:TPU:1, one launch (start us, length us, event | category | flops | bytes accessed | tf_op | source)
XLA Modules:
  0.0 197.3 jit_solution(2849267742111296669)
XLA Ops:
  6.8 3.3 %collective-permute-start.1 = (f32[16,2048]{1,0:T(8,128)S(1)}, f32[16,2048]{1,0:T(8,128)S(1)}, u32[]{:S(2)}, u32[]{:S(2)}) collective-permute-start(f32[16,2048]{1,0:T(8,128)S(1)} %get-tuple-element.27), channel_id=1, source_target_pairs={{0,64},{1,65},{2,66},{3,67},{4,68},{5,69},{6,70},{7,71},{8,72},{9,... | collective-permute-start | bytes 393224 | tf_op jit(solution)/shard_map/ppermute | solution.py:36
  10.9 2.7 %collective-permute-start.3 = (f32[16,2048]{1,0:T(8,128)S(1)}, f32[16,2048]{1,0:T(8,128)S(1)}, u32[]{:S(2)}, u32[]{:S(2)}) collective-permute-start(f32[16,2048]{1,0:T(8,128)S(1)} %get-tuple-element.29), channel_id=1, source_target_pairs={{0,24},{1,25},{2,26},{3,27},{4,28},{5,29},{6,30},{7,31},{8,16},{9,... | collective-permute-start | bytes 393224 | tf_op jit(solution)/shard_map/ppermute | solution.py:36
  14.3 2.2 %collective-permute-done.1.refs_2_ = f32[16,2048]{1,0:T(8,128)S(1)} collective-permute-done((f32[16,2048]{1,0:T(8,128)S(1)}, f32[16,2048]{1,0:T(8,128)S(1)}, u32[]{:S(2)}, u32[]{:S(2)}) %collective-permute-start.1) | collective-permute-done | bytes 131104 | tf_op jit(solution)/shard_map/ppermute | solution.py:36
  16.5 2.3 %collective-permute-start.5 = (f32[16,2048]{1,0:T(8,128)S(1)}, f32[16,2048]{1,0:T(8,128)S(1)}, u32[]{:S(2)}, u32[]{:S(2)}) collective-permute-start(f32[16,2048]{1,0:T(8,128)S(1)} %get-tuple-element.31), channel_id=1, source_target_pairs={{0,88},{1,89},{2,90},{3,91},{4,92},{5,93},{6,94},{7,95},{8,80},{9,... | collective-permute-start | bytes 393224 | tf_op jit(solution)/shard_map/ppermute | solution.py:36
  21.0 3.4 %collective-permute-done.5.refs_6_ = f32[16,2048]{1,0:T(8,128)S(1)} collective-permute-done((f32[16,2048]{1,0:T(8,128)S(1)}, f32[16,2048]{1,0:T(8,128)S(1)}, u32[]{:S(2)}, u32[]{:S(2)}) %collective-permute-start.5) | collective-permute-done | bytes 131104 | tf_op jit(solution)/shard_map/ppermute | solution.py:36
  26.5 2.5 %collective-permute-start.29 = (f32[128,2048]{1,0:T(8,128)S(1)}, f32[128,2048]{1,0:T(8,128)S(1)}, u32[]{:S(2)}, u32[]{:S(2)}) collective-permute-start(f32[128,2048]{1,0:T(8,128)S(1)} %shard_map.65.refs_0_), channel_id=1, source_target_pairs={{0,2},{1,7},{2,4},{3,1},{4,6},{5,3},{6,0},{7,5},{8,10},{9,15},{10,... | collective-permute-start | bytes 3145736 | tf_op jit(solution)/shard_map/ppermute | solution.py:36
  29.4 3.7 %collective-permute-start.17 = (f32[2,16,1024]{2,1,0:T(8,128)S(1)}, f32[2,16,1024]{2,1,0:T(8,128)S(1)}, u32[]{:S(2)}, u32[]{:S(2)}) collective-permute-start(f32[2,16,1024]{2,1,0:T(8,128)S(1)} %get-tuple-element.37), channel_id=1, source_target_pairs={{0,4},{1,5},{2,6},{3,7},{4,0},{5,1},{6,2},{7,3},{8,12},{9,13},{10,... | collective-permute-start | bytes 393224 | tf_op jit(solution)/shard_map/ppermute | solution.py:36
  33.0 27.1 %collective-permute-done.16.refs_1_ = f32[2,16,1024]{2,1,0:T(8,128)S(1)} collective-permute-done((f32[2,16,1024]{2,1,0:T(8,128)S(1)}, f32[2,16,1024]{2,1,0:T(8,128)S(1)}, u32[]{:S(2)}, u32[]{:S(2)}) %collective-permute-start.16) | collective-permute-done | bytes 131104 | tf_op jit(solution)/shard_map/ppermute | solution.py:36
  60.1 2.4 %collective-permute-start.19 = (f32[2,16,1024]{2,1,0:T(8,128)S(1)}, f32[2,16,1024]{2,1,0:T(8,128)S(1)}, u32[]{:S(2)}, u32[]{:S(2)}) collective-permute-start(f32[2,16,1024]{2,1,0:T(8,128)S(1)} %get-tuple-element.39), channel_id=1, source_target_pairs={{0,24},{1,25},{2,26},{3,27},{4,28},{5,29},{6,30},{7,31},{8,16},{9,... | collective-permute-start | bytes 393224 | tf_op jit(solution)/shard_map/ppermute | solution.py:36
  62.6 2.7 %collective-permute-start.21 = (f32[2,16,1024]{2,1,0:T(8,128)S(1)}, f32[2,16,1024]{2,1,0:T(8,128)S(1)}, u32[]{:S(2)}, u32[]{:S(2)}) collective-permute-start(f32[2,16,1024]{2,1,0:T(8,128)S(1)} %get-tuple-element.41), channel_id=1, source_target_pairs={{0,28},{1,29},{2,30},{3,31},{4,24},{5,25},{6,26},{7,27},{8,20},{9,... | collective-permute-start | bytes 393224 | tf_op jit(solution)/shard_map/ppermute | solution.py:36
  66.5 4.1 %collective-permute-start.22 = (f32[2,16,1024]{2,1,0:T(8,128)S(1)}, f32[2,16,1024]{2,1,0:T(8,128)S(1)}, u32[]{:S(2)}, u32[]{:S(2)}) collective-permute-start(f32[2,16,1024]{2,1,0:T(8,128)S(1)} %get-tuple-element.42), channel_id=1, source_target_pairs={{0,30},{1,31},{2,24},{3,25},{4,26},{5,27},{6,28},{7,29},{8,22},{9,... | collective-permute-start | bytes 393224 | tf_op jit(solution)/shard_map/ppermute | solution.py:36
  70.6 3.9 %collective-permute-done.20.refs_5_ = f32[2,16,1024]{2,1,0:T(8,128)S(1)} collective-permute-done((f32[2,16,1024]{2,1,0:T(8,128)S(1)}, f32[2,16,1024]{2,1,0:T(8,128)S(1)}, u32[]{:S(2)}, u32[]{:S(2)}) %collective-permute-start.20) | collective-permute-done | bytes 131104 | tf_op jit(solution)/shard_map/ppermute | solution.py:36
  79.8 4.1 %collective-permute-start.33 = (f32[128,2048]{1,0:T(8,128)S(1)}, f32[128,2048]{1,0:T(8,128)S(1)}, u32[]{:S(2)}, u32[]{:S(2)}) collective-permute-start(f32[128,2048]{1,0:T(8,128)S(1)} %collective-permute-done.29.refs_1_), channel_id=1, source_target_pairs={{0,1},{1,0},{2,3},{3,2},{4,5},{5,4},{6,7},{7,6},{8,9},{9,8},{10,11... | collective-permute-start | bytes 3145736 | tf_op jit(solution)/shard_map/ppermute | solution.py:36
  83.9 16.8 %collective-permute-done.7.refs_0_ = f32[128,2048]{1,0:T(8,128)S(1)} collective-permute-done((f32[128,2048]{1,0:T(8,128)S(1)}, f32[128,2048]{1,0:T(8,128)S(1)}, u32[]{:S(2)}, u32[]{:S(2)}) %collective-permute-start.7) | collective-permute-done | bytes 1048608 | tf_op jit(solution)/shard_map/ppermute | solution.py:36
  102.9 20.7 %collective-permute-done.23.refs_6_.refs_8_ = f32[256,1024]{1,0:T(8,128)S(1)} collective-permute-done((f32[256,1024]{1,0:T(8,128)S(1)}, f32[256,1024]{1,0:T(8,128)S(1)}, u32[]{:S(2)}, u32[]{:S(2)}) %collective-permute-start.23) | collective-permute-done | bytes 1048608 | tf_op jit(solution)/shard_map/ppermute | solution.py:36
  128.4 8.1 %collective-permute-start.35 = (f32[128,2048]{1,0:T(8,128)S(1)}, f32[128,2048]{1,0:T(8,128)S(1)}, u32[]{:S(2)}, u32[]{:S(2)}) collective-permute-start(f32[128,2048]{1,0:T(8,128)S(1)} %collective-permute-done.31.refs_3_), channel_id=1, source_target_pairs={{0,1},{1,0},{2,3},{3,2},{4,5},{5,4},{6,7},{7,6},{8,9},{9,8},{10,11... | collective-permute-start | bytes 3145736 | tf_op jit(solution)/shard_map/ppermute | solution.py:36
  136.5 6.5 %collective-permute-done.9.refs_2_ = f32[128,2048]{1,0:T(8,128)S(1)} collective-permute-done((f32[128,2048]{1,0:T(8,128)S(1)}, f32[128,2048]{1,0:T(8,128)S(1)}, u32[]{:S(2)}, u32[]{:S(2)}) %collective-permute-start.9) | collective-permute-done | bytes 1048608 | tf_op jit(solution)/shard_map/ppermute | solution.py:36
  144.9 5.7 %shard_map.68 = (f32[8,2048]{1,0:T(8,128)S(1)}, f32[8,1024]{1,0:T(8,128)S(1)}) custom-call(s32[8]{0:T(128)S(1)} %stack.39.spot, s32[1,8192]{1,0:T(1,128)S(1)} %bitcast.12, f32[1,8192]{1,0:T(1,128)S(1)} %bitcast.13), custom_call_target="tpu_custom_call" | custom-call | flops 1073741824 | bytes 1048576 | tf_op jit(solution)/shard_map/pallas_call | solution.py:40
  152.1 9.6 %shard_map.69.refs_12_ = f32[2048,1024]{1,0:T(8,128)S(1)} custom-call(s32[8]{0:T(128)S(1)} %stack.39.spot, f32[128,2048]{1,0:T(8,128)S(1)} %shard_map.65.refs_0_, f32[128,2048]{1,0:T(8,128)S(1)} %collective-permute-done.29.refs_1_, f32[128,2048]{1,0:T(8,128)S(1)} %collective-permute-done.30.refs_2_, f32[128,2048]{1,0:T(8,128)S(1)} %collective-permute-done.32.refs_3_.refs_4_, ...), custom_call_target="tpu_custom_call" | custom-call | flops 6442450944 | bytes 25165824 | tf_op jit(solution)/shard_map/pallas_call | solution.py:40
  161.7 2.9 %collective-permute-start.28 = (f32[256,1024]{1,0:T(8,128)S(1)}, f32[256,1024]{1,0:T(8,128)S(1)}, u32[]{:S(2)}, u32[]{:S(2)}) collective-permute-start(f32[256,1024]{1,0:T(8,128)S(1)} %collective-permute-done.27.refs_11_), channel_id=1, source_target_pairs={{0,16},{1,17},{2,18},{3,19},{4,20},{5,21},{6,22},{7,23},{8,24},{9,... | collective-permute-start | bytes 3145736 | tf_op jit(solution)/shard_map/ppermute | solution.py:36
  164.9 8.1 %shard_map.70.refs_9_ = f32[2048,1024]{1,0:T(8,128)S(1)} custom-call(s32[8]{0:T(128)S(1)} %stack.39.spot, f32[128,2048]{1,0:T(8,128)S(1)} %shard_map.65.refs_0_, f32[128,2048]{1,0:T(8,128)S(1)} %collective-permute-done.29.refs_1_, f32[128,2048]{1,0:T(8,128)S(1)} %collective-permute-done.30.refs_2_, ...), custom_call_target="tpu_custom_call", output_to_operand_aliasing={{}: (13, {})} | custom-call | flops 6442450944 | bytes 25165824 | tf_op jit(solution)/shard_map/pallas_call | solution.py:40
  173.0 8.1 %shard_map.71.refs_12_ = f32[2048,1024]{1,0:T(8,128)S(1)} custom-call(s32[8]{0:T(128)S(1)} %stack.39.spot, f32[128,2048]{1,0:T(8,128)S(1)} %collective-permute-done.7.refs_0_, f32[128,2048]{1,0:T(8,128)S(1)} %collective-permute-done.8.refs_1_, f32[128,2048]{1,0:T(8,128)S(1)} %collective-permute-done.9.refs_2_, ...), custom_call_target="tpu_custom_call", output_to_operand_aliasing={{}: (10, {})} | custom-call | flops 6442450944 | bytes 25165824 | tf_op jit(solution)/shard_map/pallas_call | solution.py:40
  181.1 6.9 %collective-permute-done.28.refs_11_ = f32[256,1024]{1,0:T(8,128)S(1)} collective-permute-done((f32[256,1024]{1,0:T(8,128)S(1)}, f32[256,1024]{1,0:T(8,128)S(1)}, u32[]{:S(2)}, u32[]{:S(2)}) %collective-permute-start.28) | collective-permute-done | bytes 1048608 | tf_op jit(solution)/shard_map/ppermute | solution.py:36
  188.0 9.0 %shard_map.72 = f32[2048,1024]{1,0:T(8,128)} custom-call(s32[8]{0:T(128)S(1)} %stack.39.spot, f32[128,2048]{1,0:T(8,128)S(1)} %collective-permute-done.7.refs_0_, f32[128,2048]{1,0:T(8,128)S(1)} %collective-permute-done.8.refs_1_, f32[128,2048]{1,0:T(8,128)S(1)} %collective-permute-done.9.refs_2_, f32[128,2048]{1,0:T(8,128)S(1)} %collective-permute-done.10.refs_3_, ...), custom_call_target="tpu_custom_call" | custom-call | flops 6442450944 | bytes 25165824 | tf_op jit(solution)/shard_map/pallas_call | solution.py:40
  (69 shorter events, 30.0 us)
Async XLA Ops:
  3.6 25.4 %collective-permute-start.15 = (f32[8,16,1024]{2,1,0:T(8,128)S(1)}, f32[8,16,1024]{2,1,0:T(8,128)S(1)}, u32[]{:S(2)}, u32[]{:S(2)}) collective-permute-start(f32[8,16,1024]{2,1,0:T(8,128)S(1)} %get-tuple-element.34), channel_id=1, source_target_pairs={{0,1},{1,0},{2,3},{3,2},{4,5},{5,4},{6,7},{7,6},{8,9},{9,8},{10,11... | collective-permute-start | bytes 1572872 | tf_op jit(solution)/shard_map/ppermute | solution.py:36
  26.5 51.7 %collective-permute-start.29 = (f32[128,2048]{1,0:T(8,128)S(1)}, f32[128,2048]{1,0:T(8,128)S(1)}, u32[]{:S(2)}, u32[]{:S(2)}) collective-permute-start(f32[128,2048]{1,0:T(8,128)S(1)} %shard_map.65.refs_0_), channel_id=1, source_target_pairs={{0,2},{1,7},{2,4},{3,1},{4,6},{5,3},{6,0},{7,5},{8,10},{9,15},{10,... | collective-permute-start | bytes 3145736 | tf_op jit(solution)/shard_map/ppermute | solution.py:36
  29.0 49.1 %collective-permute-start.30 = (f32[128,2048]{1,0:T(8,128)S(1)}, f32[128,2048]{1,0:T(8,128)S(1)}, u32[]{:S(2)}, u32[]{:S(2)}) collective-permute-start(f32[128,2048]{1,0:T(8,128)S(1)} %shard_map.65.refs_0_), channel_id=1, source_target_pairs={{0,6},{1,3},{2,0},{3,5},{4,2},{5,7},{6,4},{7,1},{8,14},{9,11},{10,... | collective-permute-start | bytes 3145736 | tf_op jit(solution)/shard_map/ppermute | solution.py:36
  29.1 31.0 %collective-permute-start.16 = (f32[2,16,1024]{2,1,0:T(8,128)S(1)}, f32[2,16,1024]{2,1,0:T(8,128)S(1)}, u32[]{:S(2)}, u32[]{:S(2)}) collective-permute-start(f32[2,16,1024]{2,1,0:T(8,128)S(1)} %get-tuple-element.36), channel_id=1, source_target_pairs={{0,2},{1,3},{2,4},{3,5},{4,6},{5,7},{6,0},{7,1},{8,10},{9,11},{10,... | collective-permute-start | bytes 393224 | tf_op jit(solution)/shard_map/ppermute | solution.py:36
  29.4 33.2 %collective-permute-start.17 = (f32[2,16,1024]{2,1,0:T(8,128)S(1)}, f32[2,16,1024]{2,1,0:T(8,128)S(1)}, u32[]{:S(2)}, u32[]{:S(2)}) collective-permute-start(f32[2,16,1024]{2,1,0:T(8,128)S(1)} %get-tuple-element.37), channel_id=1, source_target_pairs={{0,4},{1,5},{2,6},{3,7},{4,0},{5,1},{6,2},{7,3},{8,12},{9,13},{10,... | collective-permute-start | bytes 393224 | tf_op jit(solution)/shard_map/ppermute | solution.py:36
  33.0 29.6 %collective-permute-start.18 = (f32[2,16,1024]{2,1,0:T(8,128)S(1)}, f32[2,16,1024]{2,1,0:T(8,128)S(1)}, u32[]{:S(2)}, u32[]{:S(2)}) collective-permute-start(f32[2,16,1024]{2,1,0:T(8,128)S(1)} %get-tuple-element.38), channel_id=1, source_target_pairs={{0,6},{1,7},{2,0},{3,1},{4,2},{5,3},{6,4},{7,5},{8,14},{9,15},{10,... | collective-permute-start | bytes 393224 | tf_op jit(solution)/shard_map/ppermute | solution.py:36
  76.0 24.7 %collective-permute-start.7 = (f32[128,2048]{1,0:T(8,128)S(1)}, f32[128,2048]{1,0:T(8,128)S(1)}, u32[]{:S(2)}, u32[]{:S(2)}) collective-permute-start(f32[128,2048]{1,0:T(8,128)S(1)} %shard_map.65.refs_0_), channel_id=1, source_target_pairs={{0,8},{1,9},{2,10},{3,11},{4,12},{5,13},{6,14},{7,15},{8,0},{9,1},... | collective-permute-start | bytes 3145736 | tf_op jit(solution)/shard_map/ppermute | solution.py:36
  76.1 26.0 %collective-permute-start.26 = (f32[256,1024]{1,0:T(8,128)S(1)}, f32[256,1024]{1,0:T(8,128)S(1)}, u32[]{:S(2)}, u32[]{:S(2)}) collective-permute-start(f32[256,1024]{1,0:T(8,128)S(1)} %shard_map.67.refs_6_.refs_8_), channel_id=1, source_target_pairs={{0,32},{1,97},{2,34},{3,99},{4,36},{5,101},{6,38},{7,103},{8,40},{... | collective-permute-start | bytes 3145736 | tf_op jit(solution)/shard_map/ppermute | solution.py:36
  78.2 23.9 %collective-permute-start.36 = (f32[256,1024]{1,0:T(8,128)S(1)}, f32[256,1024]{1,0:T(8,128)S(1)}, u32[]{:S(2)}, u32[]{:S(2)}) collective-permute-start(f32[256,1024]{1,0:T(8,128)S(1)} %shard_map.67.refs_6_.refs_8_), channel_id=1, source_target_pairs={{0,96},{1,33},{2,98},{3,35},{4,100},{5,37},{6,102},{7,39},{8,104},... | collective-permute-start | bytes 3145736 | tf_op jit(solution)/shard_map/ppermute | solution.py:36
  78.2 45.4 %collective-permute-start.23 = (f32[256,1024]{1,0:T(8,128)S(1)}, f32[256,1024]{1,0:T(8,128)S(1)}, u32[]{:S(2)}, u32[]{:S(2)}) collective-permute-start(f32[256,1024]{1,0:T(8,128)S(1)} %shard_map.67.refs_6_.refs_8_), channel_id=1, source_target_pairs={{0,16},{1,17},{2,18},{3,19},{4,20},{5,21},{6,22},{7,23},{8,24},{9,... | collective-permute-start | bytes 3145736 | tf_op jit(solution)/shard_map/ppermute | solution.py:36
  79.8 44.5 %collective-permute-start.33 = (f32[128,2048]{1,0:T(8,128)S(1)}, f32[128,2048]{1,0:T(8,128)S(1)}, u32[]{:S(2)}, u32[]{:S(2)}) collective-permute-start(f32[128,2048]{1,0:T(8,128)S(1)} %collective-permute-done.29.refs_1_), channel_id=1, source_target_pairs={{0,1},{1,0},{2,3},{3,2},{4,5},{5,4},{6,7},{7,6},{8,9},{9,8},{10,11... | collective-permute-start | bytes 3145736 | tf_op jit(solution)/shard_map/ppermute | solution.py:36
  100.8 23.8 %collective-permute-start.34 = (f32[128,2048]{1,0:T(8,128)S(1)}, f32[128,2048]{1,0:T(8,128)S(1)}, u32[]{:S(2)}, u32[]{:S(2)}) collective-permute-start(f32[128,2048]{1,0:T(8,128)S(1)} %collective-permute-done.30.refs_2_), channel_id=1, source_target_pairs={{0,1},{1,0},{2,3},{3,2},{4,5},{5,4},{6,7},{7,6},{8,9},{9,8},{10,11... | collective-permute-start | bytes 3145736 | tf_op jit(solution)/shard_map/ppermute | solution.py:36
  102.1 24.1 %collective-permute-start.31 = (f32[128,2048]{1,0:T(8,128)S(1)}, f32[128,2048]{1,0:T(8,128)S(1)}, u32[]{:S(2)}, u32[]{:S(2)}) collective-permute-start(f32[128,2048]{1,0:T(8,128)S(1)} %collective-permute-done.29.refs_1_), channel_id=1, source_target_pairs={{0,2},{1,7},{2,4},{3,1},{4,6},{5,3},{6,0},{7,5},{8,10},{9,15},{10,... | collective-permute-start | bytes 3145736 | tf_op jit(solution)/shard_map/ppermute | solution.py:36
  102.1 26.3 %collective-permute-start.8 = (f32[128,2048]{1,0:T(8,128)S(1)}, f32[128,2048]{1,0:T(8,128)S(1)}, u32[]{:S(2)}, u32[]{:S(2)}) collective-permute-start(f32[128,2048]{1,0:T(8,128)S(1)} %collective-permute-done.7.refs_0_), channel_id=1, source_target_pairs={{0,2},{1,7},{2,4},{3,1},{4,6},{5,3},{6,0},{7,5},{8,10},{9,15},{10,... | collective-permute-start | bytes 3145736 | tf_op jit(solution)/shard_map/ppermute | solution.py:36
  124.3 26.3 %collective-permute-start.11 = (f32[128,2048]{1,0:T(8,128)S(1)}, f32[128,2048]{1,0:T(8,128)S(1)}, u32[]{:S(2)}, u32[]{:S(2)}) collective-permute-start(f32[128,2048]{1,0:T(8,128)S(1)} %collective-permute-done.7.refs_0_), channel_id=1, source_target_pairs={{0,1},{1,0},{2,3},{3,2},{4,5},{5,4},{6,7},{7,6},{8,9},{9,8},{10,11... | collective-permute-start | bytes 3145736 | tf_op jit(solution)/shard_map/ppermute | solution.py:36
  124.5 26.2 %collective-permute-start.27 = (f32[256,1024]{1,0:T(8,128)S(1)}, f32[256,1024]{1,0:T(8,128)S(1)}, u32[]{:S(2)}, u32[]{:S(2)}) collective-permute-start(f32[256,1024]{1,0:T(8,128)S(1)} %collective-permute-done.26.refs_7_.refs_9_), channel_id=1, source_target_pairs={{0,32},{1,97},{2,34},{3,99},{4,36},{5,101},{6,38},{7,103},{8,40},{... | collective-permute-start | bytes 3145736 | tf_op jit(solution)/shard_map/ppermute | solution.py:36
  126.2 24.7 %collective-permute-start.24 = (f32[256,1024]{1,0:T(8,128)S(1)}, f32[256,1024]{1,0:T(8,128)S(1)}, u32[]{:S(2)}, u32[]{:S(2)}) collective-permute-start(f32[256,1024]{1,0:T(8,128)S(1)} %collective-permute-done.23.refs_6_.refs_8_), channel_id=1, source_target_pairs={{0,32},{1,97},{2,34},{3,99},{4,36},{5,101},{6,38},{7,103},{8,40},{... | collective-permute-start | bytes 3145736 | tf_op jit(solution)/shard_map/ppermute | solution.py:36
  128.4 33.3 %collective-permute-start.35 = (f32[128,2048]{1,0:T(8,128)S(1)}, f32[128,2048]{1,0:T(8,128)S(1)}, u32[]{:S(2)}, u32[]{:S(2)}) collective-permute-start(f32[128,2048]{1,0:T(8,128)S(1)} %collective-permute-done.31.refs_3_), channel_id=1, source_target_pairs={{0,1},{1,0},{2,3},{3,2},{4,5},{5,4},{6,7},{7,6},{8,9},{9,8},{10,11... | collective-permute-start | bytes 3145736 | tf_op jit(solution)/shard_map/ppermute | solution.py:36
  143.0 21.6 %collective-permute-start.10 = (f32[128,2048]{1,0:T(8,128)S(1)}, f32[128,2048]{1,0:T(8,128)S(1)}, u32[]{:S(2)}, u32[]{:S(2)}) collective-permute-start(f32[128,2048]{1,0:T(8,128)S(1)} %collective-permute-done.8.refs_1_), channel_id=1, source_target_pairs={{0,2},{1,7},{2,4},{3,1},{4,6},{5,3},{6,0},{7,5},{8,10},{9,15},{10,... | collective-permute-start | bytes 3145736 | tf_op jit(solution)/shard_map/ppermute | solution.py:36
  150.7 22.3 %collective-permute-start.25 = (f32[256,1024]{1,0:T(8,128)S(1)}, f32[256,1024]{1,0:T(8,128)S(1)}, u32[]{:S(2)}, u32[]{:S(2)}) collective-permute-start(f32[256,1024]{1,0:T(8,128)S(1)} %collective-permute-done.23.refs_6_.refs_8_), channel_id=1, source_target_pairs={{0,96},{1,33},{2,98},{3,35},{4,100},{5,37},{6,102},{7,39},{8,104},... | collective-permute-start | bytes 3145736 | tf_op jit(solution)/shard_map/ppermute | solution.py:36
  150.7 22.2 %collective-permute-start.12 = (f32[128,2048]{1,0:T(8,128)S(1)}, f32[128,2048]{1,0:T(8,128)S(1)}, u32[]{:S(2)}, u32[]{:S(2)}) collective-permute-start(f32[128,2048]{1,0:T(8,128)S(1)} %collective-permute-done.8.refs_1_), channel_id=1, source_target_pairs={{0,1},{1,0},{2,3},{3,2},{4,5},{5,4},{6,7},{7,6},{8,9},{9,8},{10,11... | collective-permute-start | bytes 3145736 | tf_op jit(solution)/shard_map/ppermute | solution.py:36
  150.9 22.1 %collective-permute-start.13 = (f32[128,2048]{1,0:T(8,128)S(1)}, f32[128,2048]{1,0:T(8,128)S(1)}, u32[]{:S(2)}, u32[]{:S(2)}) collective-permute-start(f32[128,2048]{1,0:T(8,128)S(1)} %collective-permute-done.9.refs_2_), channel_id=1, source_target_pairs={{0,1},{1,0},{2,3},{3,2},{4,5},{5,4},{6,7},{7,6},{8,9},{9,8},{10,11... | collective-permute-start | bytes 3145736 | tf_op jit(solution)/shard_map/ppermute | solution.py:36
  161.7 26.3 %collective-permute-start.28 = (f32[256,1024]{1,0:T(8,128)S(1)}, f32[256,1024]{1,0:T(8,128)S(1)}, u32[]{:S(2)}, u32[]{:S(2)}) collective-permute-start(f32[256,1024]{1,0:T(8,128)S(1)} %collective-permute-done.27.refs_11_), channel_id=1, source_target_pairs={{0,16},{1,17},{2,18},{3,19},{4,20},{5,21},{6,22},{7,23},{8,24},{9,... | collective-permute-start | bytes 3145736 | tf_op jit(solution)/shard_map/ppermute | solution.py:36
  164.6 23.4 %collective-permute-start.14 = (f32[128,2048]{1,0:T(8,128)S(1)}, f32[128,2048]{1,0:T(8,128)S(1)}, u32[]{:S(2)}, u32[]{:S(2)}) collective-permute-start(f32[128,2048]{1,0:T(8,128)S(1)} %collective-permute-done.10.refs_3_), channel_id=1, source_target_pairs={{0,1},{1,0},{2,3},{3,2},{4,5},{5,4},{6,7},{7,6},{8,9},{9,8},{10,11... | collective-permute-start | bytes 3145736 | tf_op jit(solution)/shard_map/ppermute | solution.py:36
  (16 other events, 128.6 us)

commit v3 on v2

--- a/solution.py
+++ b/solution.py
@@ -57,14 +57,10 @@
 HBM = pl.BlockSpec(memory_space=pltpu.HBM)
 
 
-def scale_body(spot, green, pack, *outs):
+def scale_body(spot, green, weight, *outs):
     row_pieces, mine, theirs = outs[:8], outs[8], outs[9]
     z, y_hi, y_lo, x, core = (spot[i] for i in range(5))
-    noise, chosen = pack[0:1, 0:16], pack[0:1, 16:32]
-    factor = jnp.zeros_like(noise)
-    for s in range(4):
-        factor = jnp.where(chosen == float(s), pack[0:1, 32 + s : 33 + s], factor)
-    root = jnp.broadcast_to(jnp.sqrt(noise * factor), (16, 16))
+    root = jnp.broadcast_to(jnp.sqrt(weight[...]), (16, 16))
     eye = lax.broadcasted_iota(jnp.int32, (16, 16), 0) == lax.broadcasted_iota(jnp.int32, (16, 16), 1)
     root = jnp.sum(jnp.where(eye, root, 0.0), axis=1, keepdims=True)
     for c in range(2):
@@ -157,44 +153,45 @@
     return jnp.where(spacing == 0.0, sides[:, 3:4], coupling)
 
 
-EARLY = ((0, 1, 3), (0, 1, 3), (0, 1, 3), (), (0, 1, 3), (1, 3), (1, 3), ())
-REST = ((2,), (2,), (2,), (0, 1, 2, 3), (2,), (0, 2), (0, 2), (0, 1, 2, 3))
+EARLY = ((0, 1, 2), (0, 1, 2), (0, 1, 2), (), (0, 1, 2), (1, 2), (1, 2), ())
+REST = ((3,), (3,), (3,), (0, 1, 2, 3), (3,), (0, 3), (0, 3), (0, 1, 2, 3))
+LATE = ((0, 1), (0, 1), (0, 1), (), (0, 1), (), (), ())
+LATER = ((2, 3), (2, 3), (2, 3), (), (2, 3), (0, 1, 2, 3), (0, 1, 2, 3), ())
+LAST = ((), (), (), (0, 1, 2, 3), (), (), (), (0, 1, 2, 3))
 TILE = 256
 
 
+def offsets(core):
+    return (0, 1 + 2 * core, 3 - 2 * core, 2)
+
+
+def blocks_of(plan):
+    return sorted(set(sum(plan, ())))
+
+
 def split_right(late, plan, core, right, high, low):
-    start = 0
+    refs = dict(zip(blocks_of(plan), right))
+    target = 0
     for i, chosen in enumerate(plan):
-        who = core if i < 4 else 1 - core
-        dx = (0, 1 + 2 * who, 3 - 2 * who, 2)[i % 4]
-        at = {dz: start + 32 * k for k, dz in enumerate(chosen)}
-        targets = []
-        if 0 in at:
-            targets.append((0, at[0]))
-        if 1 in at:
-            targets.append((1, at[1] + core * (at[3] - at[1])))
-            targets.append((2, at[3] + core * (at[1] - at[3])))
-        if 2 in at:
-            targets.append((3, at[2]))
-        for m, base in targets:
+        dx = offsets(core if i < 4 else 1 - core)[i % 4]
+        for m in chosen:
             for c in range(2):
                 c_from = 1 - c if late else c
                 source = pl.multiple_of(dx * 64 + c_from * 32 + i // 4 * 16, 16)
-                target = pl.multiple_of(base + c * 16, 16)
-                piece = right[m][pl.ds(source, 16), :]
+                piece = refs[m][pl.ds(source, 16), :]
                 top = piece.astype(jnp.bfloat16)
-                high[pl.ds(target, 16), :] = top
-                low[pl.ds(target, 16), :] = (piece - top.astype(jnp.float32)).astype(jnp.bfloat16)
-        start += 32 * len(chosen)
-
-
-def product(left, plan, part, high, low):
+                high[target : target + 16, :] = top
+                low[target : target + 16, :] = (piece - top.astype(jnp.float32)).astype(jnp.bfloat16)
+                target += 16
+
+
+def product(core, left, plan, part, high, low):
     refs = iter(left)
     rows = []
     for chosen in plan:
         if chosen:
             ref = next(refs)
-            rows += [ref[dz * 32 : dz * 32 + 32, part] for dz in chosen]
+            rows += [ref[pl.ds(pl.multiple_of(offsets(core)[m] * 32, 32), 32), part] for m in chosen]
     block = jnp.concatenate(rows, 0).T
     top = block.astype(jnp.bfloat16)
     rest = (block - top.astype(jnp.float32)).astype(jnp.bfloat16)
@@ -207,7 +204,7 @@
 
 def gram_body(plan, late, last, spot, *refs):
     n_left = sum(1 for chosen in plan if chosen)
-    n_right = 3 if plan is EARLY else 4
+    n_right = len(blocks_of(plan))
     left, right = refs[:n_left], refs[n_left : n_left + n_right]
     if last:
         *extra, result, high, low, out, sent = refs[n_left + n_right :]
@@ -219,10 +216,10 @@
         part = pl.ds(pl.multiple_of(i * TILE, TILE), TILE)
         return pltpu.make_async_copy(out.at[part, :], result.at[part, :], sent.at[i])
 
-    @pl.loop(0, ROWS // TILE, unroll=UNROLL)
+    @pl.loop(0, ROWS // TILE, unroll=8 if plan in (LATER, LAST) else UNROLL)
     def _(i):
         part = pl.ds(pl.multiple_of(i * TILE, TILE), TILE)
-        block = product(left, plan, part, high, low)
+        block = product(spot[4], left, plan, part, high, low)
         if len(extra) == 1:
             out[part, :] = extra[0][part, :] + block
         else:
@@ -240,7 +237,7 @@
 
 def gram_call(plan, late, last, spot, left, right, extra):
     left = [ref for ref, chosen in zip(left, plan) if chosen]
-    right = right[:3] if plan is EARLY else right
+    right = [right[m] for m in blocks_of(plan)]
     depth = 32 * sum(len(chosen) for chosen in plan)
     args = (spot, *left, *right, *extra)
     options = {}
@@ -315,11 +312,12 @@
             (row_start // PATCHES == col_start // PATCHES).astype(jnp.int32),
         ]
     ).astype(jnp.int32)
-    pack = jnp.concatenate([noise_precision, data_set.astype(jnp.float32), set_scale, jnp.zeros((92,), jnp.float32)])
+    matches = data_set[:, None] == jnp.arange(set_scale.shape[0], dtype=jnp.int32)[None, :]
+    weight = jnp.sum(jnp.where(matches, noise_precision[:, None] * set_scale[None, :], 0.0), axis=1)
     *row_pieces, mine, theirs = kernel_call(
         scale_body,
         [shape(16, 2048)] * 8 + [shape(8, 16, 1024)] * 2,
-        (spot, green, pack.reshape(1, -1)),
+        (spot, green, weight.reshape(1, 16)),
         in_specs=[SMEM, VMEM, VMEM],
         flops=1 << 20,
         nbytes=3 << 20,
@@ -348,8 +346,9 @@
     total = gram_call(EARLY, False, False, spot, left, col_near, sides)
     total = gram_call(REST, False, False, spot, left, col_near, [total])
     left = row_late + swap(row_late)
-    total = gram_call(EARLY, True, False, spot, left, col_late, [total])
-    return gram_call(REST, True, True, spot, left, col_late, [total])
+    total = gram_call(LATE, True, False, spot, left, col_late, [total])
+    total = gram_call(LATER, True, False, spot, left, col_late, [total])
+    return gram_call(LAST, True, True, spot, left, col_late, [total])
 
 
 def solution(mesh):

time: 199 us -> 194 us (0.975)
  waiting for transfers between devices: 92.4 us -> 84.9 us
    ppermute x37, waiting for transfers between devices: 92.4 us -> 84.9 us  [send(): return lax.ppermute(block, AXES, pairs)]
    pallas_call x9 -> x10, Pallas kernels: 41.7 us -> 42.2 us  [kernel_call(): pl.pallas_call(body, out_shape=outs, in_specs=in_specs or [VMEM] * len(ar...]
  transfers between devices with their start and end apart: 37 -> 37, of which waited for: 11 -> 13; matrix products, arithmetic and copies ran while one was open for 0% -> 0% of each run, Pallas kernels for 16% -> 19%
where the time goes in v3:
time: 194 us; the launch traced here: 191 us
  waiting for transfers between devices  84.9 us (44%)
  starting transfers between devices  60 us (31%)
  Pallas kernels  42.2 us (22%)
  local copies, waits for them, and re-layouts  2.83 us (1%)
    ppermute x37, waiting for transfers between devices, send(): return lax.ppermute(block, AXES, pairs)  84.9 us
    ppermute x37, starting transfers between devices, send(): return lax.ppermute(block, AXES, pairs)  60 us
    pallas_call x10, Pallas kernels, kernel_call(): pl.pallas_call(body, out_shape=outs, in_specs=in_specs or [VMEM] * len(ar...  42.2 us
  transfers between devices with their start and end apart: 37, of which 13 were waited for; matrix products, arithmetic and copies ran while one was open for 0% of the time, Pallas kernels for 19%

profile of v3, /device:TPU:1, one launch (start us, length us, event | category | flops | bytes accessed | tf_op | source)
XLA Modules:
  0.0 191.0 jit_solution(14231729258191262794)
XLA Ops:
  2.9 2.5 %collective-permute-start = (f32[16,2048]{1,0:T(8,128)S(1)}, f32[16,2048]{1,0:T(8,128)S(1)}, u32[]{:S(2)}, u32[]{:S(2)}) collective-permute-start(f32[16,2048]{1,0:T(8,128)S(1)} %get-tuple-element.26), channel_id=1, source_target_pairs={{0,32},{1,33},{2,34},{3,35},{4,36},{5,37},{6,38},{7,39},{8,40},{9,... | collective-permute-start | bytes 393224 | tf_op jit(solution)/shard_map/ppermute | solution.py:36
  5.4 3.3 %collective-permute-start.1 = (f32[16,2048]{1,0:T(8,128)S(1)}, f32[16,2048]{1,0:T(8,128)S(1)}, u32[]{:S(2)}, u32[]{:S(2)}) collective-permute-start(f32[16,2048]{1,0:T(8,128)S(1)} %get-tuple-element.27), channel_id=1, source_target_pairs={{0,64},{1,65},{2,66},{3,67},{4,68},{5,69},{6,70},{7,71},{8,72},{9,... | collective-permute-start | bytes 393224 | tf_op jit(solution)/shard_map/ppermute | solution.py:36
  9.4 2.7 %collective-permute-start.3 = (f32[16,2048]{1,0:T(8,128)S(1)}, f32[16,2048]{1,0:T(8,128)S(1)}, u32[]{:S(2)}, u32[]{:S(2)}) collective-permute-start(f32[16,2048]{1,0:T(8,128)S(1)} %get-tuple-element.29), channel_id=1, source_target_pairs={{0,24},{1,25},{2,26},{3,27},{4,28},{5,29},{6,30},{7,31},{8,16},{9,... | collective-permute-start | bytes 393224 | tf_op jit(solution)/shard_map/ppermute | solution.py:36
  12.6 2.8 %collective-permute-start.5 = (f32[16,2048]{1,0:T(8,128)S(1)}, f32[16,2048]{1,0:T(8,128)S(1)}, u32[]{:S(2)}, u32[]{:S(2)}) collective-permute-start(f32[16,2048]{1,0:T(8,128)S(1)} %get-tuple-element.31), channel_id=1, source_target_pairs={{0,88},{1,89},{2,90},{3,91},{4,92},{5,93},{6,94},{7,95},{8,80},{9,... | collective-permute-start | bytes 393224 | tf_op jit(solution)/shard_map/ppermute | solution.py:36
  21.5 2.3 %collective-permute-done.6.refs_7_ = f32[16,2048]{1,0:T(8,128)S(1)} collective-permute-done((f32[16,2048]{1,0:T(8,128)S(1)}, f32[16,2048]{1,0:T(8,128)S(1)}, u32[]{:S(2)}, u32[]{:S(2)}) %collective-permute-start.6) | collective-permute-done | bytes 131104 | tf_op jit(solution)/shard_map/ppermute | solution.py:36
  23.9 2.5 %collective-permute-start.29 = (f32[128,2048]{1,0:T(8,128)S(1)}, f32[128,2048]{1,0:T(8,128)S(1)}, u32[]{:S(2)}, u32[]{:S(2)}) collective-permute-start(f32[128,2048]{1,0:T(8,128)S(1)} %shard_map.65.refs_0_), channel_id=1, source_target_pairs={{0,2},{1,7},{2,4},{3,1},{4,6},{5,3},{6,0},{7,5},{8,10},{9,15},{10,... | collective-permute-start | bytes 3145736 | tf_op jit(solution)/shard_map/ppermute | solution.py:36
  33.8 21.7 %collective-permute-done.12.refs_1_ = f32[2,16,1024]{2,1,0:T(8,128)S(1)} collective-permute-done((f32[2,16,1024]{2,1,0:T(8,128)S(1)}, f32[2,16,1024]{2,1,0:T(8,128)S(1)}, u32[]{:S(2)}, u32[]{:S(2)}) %collective-permute-start.12) | collective-permute-done | bytes 131104 | tf_op jit(solution)/shard_map/ppermute | solution.py:36
  59.5 3.0 %collective-permute-start.17 = (f32[2,16,1024]{2,1,0:T(8,128)S(1)}, f32[2,16,1024]{2,1,0:T(8,128)S(1)}, u32[]{:S(2)}, u32[]{:S(2)}) collective-permute-start(f32[2,16,1024]{2,1,0:T(8,128)S(1)} %get-tuple-element.41), channel_id=1, source_target_pairs={{0,28},{1,29},{2,30},{3,31},{4,24},{5,25},{6,26},{7,27},{8,20},{9,... | collective-permute-start | bytes 393224 | tf_op jit(solution)/shard_map/ppermute | solution.py:36
  62.5 5.1 %collective-permute-start.18 = (f32[2,16,1024]{2,1,0:T(8,128)S(1)}, f32[2,16,1024]{2,1,0:T(8,128)S(1)}, u32[]{:S(2)}, u32[]{:S(2)}) collective-permute-start(f32[2,16,1024]{2,1,0:T(8,128)S(1)} %get-tuple-element.42), channel_id=1, source_target_pairs={{0,30},{1,31},{2,24},{3,25},{4,26},{5,27},{6,28},{7,29},{8,22},{9,... | collective-permute-start | bytes 393224 | tf_op jit(solution)/shard_map/ppermute | solution.py:36
  67.7 3.0 %collective-permute-done.16.refs_5_ = f32[2,16,1024]{2,1,0:T(8,128)S(1)} collective-permute-done((f32[2,16,1024]{2,1,0:T(8,128)S(1)}, f32[2,16,1024]{2,1,0:T(8,128)S(1)}, u32[]{:S(2)}, u32[]{:S(2)}) %collective-permute-start.16) | collective-permute-done | bytes 131104 | tf_op jit(solution)/shard_map/ppermute | solution.py:36
  73.2 2.3 %collective-permute-start.22 = (f32[256,1024]{1,0:T(8,128)S(1)}, f32[256,1024]{1,0:T(8,128)S(1)}, u32[]{:S(2)}, u32[]{:S(2)}) collective-permute-start(f32[256,1024]{1,0:T(8,128)S(1)} %shard_map.67.refs_6_.refs_8_), channel_id=1, source_target_pairs={{0,32},{1,97},{2,34},{3,99},{4,36},{5,101},{6,38},{7,103},{8,40},{... | collective-permute-start | bytes 3145736 | tf_op jit(solution)/shard_map/ppermute | solution.py:36
  75.6 3.7 %collective-permute-start.19 = (f32[256,1024]{1,0:T(8,128)S(1)}, f32[256,1024]{1,0:T(8,128)S(1)}, u32[]{:S(2)}, u32[]{:S(2)}) collective-permute-start(f32[256,1024]{1,0:T(8,128)S(1)} %shard_map.67.refs_6_.refs_8_), channel_id=1, source_target_pairs={{0,16},{1,17},{2,18},{3,19},{4,20},{5,21},{6,22},{7,23},{8,24},{9,... | collective-permute-start | bytes 3145736 | tf_op jit(solution)/shard_map/ppermute | solution.py:36
  80.8 16.2 %collective-permute-done.7.refs_0_ = f32[128,2048]{1,0:T(8,128)S(1)} collective-permute-done((f32[128,2048]{1,0:T(8,128)S(1)}, f32[128,2048]{1,0:T(8,128)S(1)}, u32[]{:S(2)}, u32[]{:S(2)}) %collective-permute-start.7) | collective-permute-done | bytes 1048608 | tf_op jit(solution)/shard_map/ppermute | solution.py:36
  98.3 2.5 %collective-permute-start.31 = (f32[128,2048]{1,0:T(8,128)S(1)}, f32[128,2048]{1,0:T(8,128)S(1)}, u32[]{:S(2)}, u32[]{:S(2)}) collective-permute-start(f32[128,2048]{1,0:T(8,128)S(1)} %collective-permute-done.29.refs_1_), channel_id=1, source_target_pairs={{0,2},{1,7},{2,4},{3,1},{4,6},{5,3},{6,0},{7,5},{8,10},{9,15},{10,... | collective-permute-start | bytes 3145736 | tf_op jit(solution)/shard_map/ppermute | solution.py:36
  101.4 21.2 %collective-permute-done.19.refs_4_.refs_6_.refs_2_ = f32[256,1024]{1,0:T(8,128)S(1)} collective-permute-done((f32[256,1024]{1,0:T(8,128)S(1)}, f32[256,1024]{1,0:T(8,128)S(1)}, u32[]{:S(2)}, u32[]{:S(2)}) %collective-permute-start.19) | collective-permute-done | bytes 1048608 | tf_op jit(solution)/shard_map/ppermute | solution.py:36
  128.2 8.2 %collective-permute-done.8.refs_1_ = f32[128,2048]{1,0:T(8,128)S(1)} collective-permute-done((f32[128,2048]{1,0:T(8,128)S(1)}, f32[128,2048]{1,0:T(8,128)S(1)}, u32[]{:S(2)}, u32[]{:S(2)}) %collective-permute-start.8) | collective-permute-done | bytes 1048608 | tf_op jit(solution)/shard_map/ppermute | solution.py:36
  139.9 5.7 %shard_map.68 = (f32[8,2048]{1,0:T(8,128)S(1)}, f32[8,1024]{1,0:T(8,128)S(1)}) custom-call(s32[8]{0:T(128)S(1)} %stack.39.spot, s32[1,8192]{1,0:T(1,128)S(1)} %bitcast.12, f32[1,8192]{1,0:T(1,128)S(1)} %bitcast.13), custom_call_target="tpu_custom_call" | custom-call | flops 1073741824 | bytes 1048576 | tf_op jit(solution)/shard_map/pallas_call | solution.py:40
  145.8 3.5 %collective-permute-start.27 = (f32[128,2048]{1,0:T(8,128)S(1)}, f32[128,2048]{1,0:T(8,128)S(1)}, u32[]{:S(2)}, u32[]{:S(2)}) collective-permute-start(f32[128,2048]{1,0:T(8,128)S(1)} %collective-permute-done.8.refs_1_), channel_id=1, source_target_pairs={{0,1},{1,0},{2,3},{3,2},{4,5},{5,4},{6,7},{7,6},{8,9},{9,8},{10,11... | collective-permute-start | bytes 3145736 | tf_op jit(solution)/shard_map/ppermute | solution.py:36
  151.4 9.5 %shard_map.69.refs_12_ = f32[2048,1024]{1,0:T(8,128)S(1)} custom-call(s32[8]{0:T(128)S(1)} %stack.39.spot, f32[128,2048]{1,0:T(8,128)S(1)} %shard_map.65.refs_0_, f32[128,2048]{1,0:T(8,128)S(1)} %collective-permute-done.29.refs_1_, f32[128,2048]{1,0:T(8,128)S(1)} %collective-permute-done.30.refs_2_, f32[128,2048]{1,0:T(8,128)S(1)} %collective-permute-done.32.refs_3_.refs_4_, ...), custom_call_target="tpu_custom_call" | custom-call | flops 6442450944 | bytes 25165824 | tf_op jit(solution)/shard_map/pallas_call | solution.py:40
  161.2 8.0 %shard_map.70.refs_6_ = f32[2048,1024]{1,0:T(8,128)S(1)} custom-call(s32[8]{0:T(128)S(1)} %stack.39.spot, f32[128,2048]{1,0:T(8,128)S(1)} %shard_map.65.refs_0_, f32[128,2048]{1,0:T(8,128)S(1)} %collective-permute-done.29.refs_1_, f32[128,2048]{1,0:T(8,128)S(1)} %collective-permute-done.30.refs_2_, ...), custom_call_target="tpu_custom_call", output_to_operand_aliasing={{}: (13, {})} | custom-call | flops 6442450944 | bytes 25165824 | tf_op jit(solution)/shard_map/pallas_call | solution.py:40
  169.2 4.8 %shard_map.71.refs_10_ = f32[2048,1024]{1,0:T(8,128)S(1)} custom-call(s32[8]{0:T(128)S(1)} %stack.39.spot, f32[128,2048]{1,0:T(8,128)S(1)} %collective-permute-done.7.refs_0_, f32[128,2048]{1,0:T(8,128)S(1)} %collective-permute-done.8.refs_1_, f32[128,2048]{1,0:T(8,128)S(1)} %collective-permute-done.25.refs_2_, ...), custom_call_target="tpu_custom_call", output_to_operand_aliasing={{}: (7, {})} | custom-call | flops 3221225472 | bytes 25165824 | tf_op jit(solution)/shard_map/pallas_call | solution.py:40
  174.0 3.6 %collective-permute-done.24.refs_9_.refs_5_ = f32[256,1024]{1,0:T(8,128)S(1)} collective-permute-done((f32[256,1024]{1,0:T(8,128)S(1)}, f32[256,1024]{1,0:T(8,128)S(1)}, u32[]{:S(2)}, u32[]{:S(2)}) %collective-permute-start.24) | collective-permute-done | bytes 1048608 | tf_op jit(solution)/shard_map/ppermute | solution.py:36
  177.6 8.0 %shard_map.72.refs_6_ = f32[2048,1024]{1,0:T(8,128)S(1)} custom-call(s32[8]{0:T(128)S(1)} %stack.39.spot, f32[128,2048]{1,0:T(8,128)S(1)} %collective-permute-done.7.refs_0_, f32[128,2048]{1,0:T(8,128)S(1)} %collective-permute-done.8.refs_1_, f32[128,2048]{1,0:T(8,128)S(1)} %collective-permute-done.25.refs_2_, ...), custom_call_target="tpu_custom_call", output_to_operand_aliasing={{}: (11, {})} | custom-call | flops 6442450944 | bytes 25165824 | tf_op jit(solution)/shard_map/pallas_call | solution.py:40
  185.6 5.2 %shard_map.73 = f32[2048,1024]{1,0:T(8,128)} custom-call(s32[8]{0:T(128)S(1)} %stack.39.spot, f32[128,2048]{1,0:T(8,128)S(1)} %collective-permute-done.9.refs_0_, f32[128,2048]{1,0:T(8,128)S(1)} %collective-permute-done.10.refs_1_, f32[256,1024]{1,0:T(8,128)S(1)} %collective-permute-done.19.refs_4_.refs_6_.refs_2_, ...), custom_call_target="tpu_custom_call" | custom-call | flops 3221225472 | bytes 25165824 | tf_op jit(solution)/shard_map/pallas_call | solution.py:40
  (68 shorter events, 39.2 us)
Async XLA Ops:
  23.9 51.7 %collective-permute-start.29 = (f32[128,2048]{1,0:T(8,128)S(1)}, f32[128,2048]{1,0:T(8,128)S(1)}, u32[]{:S(2)}, u32[]{:S(2)}) collective-permute-start(f32[128,2048]{1,0:T(8,128)S(1)} %shard_map.65.refs_0_), channel_id=1, source_target_pairs={{0,2},{1,7},{2,4},{3,1},{4,6},{5,3},{6,0},{7,5},{8,10},{9,15},{10,... | collective-permute-start | bytes 3145736 | tf_op jit(solution)/shard_map/ppermute | solution.py:36
  27.6 48.0 %collective-permute-start.30 = (f32[128,2048]{1,0:T(8,128)S(1)}, f32[128,2048]{1,0:T(8,128)S(1)}, u32[]{:S(2)}, u32[]{:S(2)}) collective-permute-start(f32[128,2048]{1,0:T(8,128)S(1)} %shard_map.65.refs_0_), channel_id=1, source_target_pairs={{0,6},{1,3},{2,0},{3,5},{4,2},{5,7},{6,4},{7,1},{8,14},{9,11},{10,... | collective-permute-start | bytes 3145736 | tf_op jit(solution)/shard_map/ppermute | solution.py:36
  29.2 26.3 %collective-permute-start.12 = (f32[2,16,1024]{2,1,0:T(8,128)S(1)}, f32[2,16,1024]{2,1,0:T(8,128)S(1)}, u32[]{:S(2)}, u32[]{:S(2)}) collective-permute-start(f32[2,16,1024]{2,1,0:T(8,128)S(1)} %get-tuple-element.36), channel_id=1, source_target_pairs={{0,2},{1,3},{2,4},{3,5},{4,6},{5,7},{6,0},{7,1},{8,10},{9,11},{10,... | collective-permute-start | bytes 393224 | tf_op jit(solution)/shard_map/ppermute | solution.py:36
  30.5 29.0 %collective-permute-start.13 = (f32[2,16,1024]{2,1,0:T(8,128)S(1)}, f32[2,16,1024]{2,1,0:T(8,128)S(1)}, u32[]{:S(2)}, u32[]{:S(2)}) collective-permute-start(f32[2,16,1024]{2,1,0:T(8,128)S(1)} %get-tuple-element.37), channel_id=1, source_target_pairs={{0,4},{1,5},{2,6},{3,7},{4,0},{5,1},{6,2},{7,3},{8,12},{9,13},{10,... | collective-permute-start | bytes 393224 | tf_op jit(solution)/shard_map/ppermute | solution.py:36
  31.9 27.6 %collective-permute-start.14 = (f32[2,16,1024]{2,1,0:T(8,128)S(1)}, f32[2,16,1024]{2,1,0:T(8,128)S(1)}, u32[]{:S(2)}, u32[]{:S(2)}) collective-permute-start(f32[2,16,1024]{2,1,0:T(8,128)S(1)} %get-tuple-element.38), channel_id=1, source_target_pairs={{0,6},{1,7},{2,0},{3,1},{4,2},{5,3},{6,4},{7,5},{8,14},{9,15},{10,... | collective-permute-start | bytes 393224 | tf_op jit(solution)/shard_map/ppermute | solution.py:36
  72.3 24.7 %collective-permute-start.7 = (f32[128,2048]{1,0:T(8,128)S(1)}, f32[128,2048]{1,0:T(8,128)S(1)}, u32[]{:S(2)}, u32[]{:S(2)}) collective-permute-start(f32[128,2048]{1,0:T(8,128)S(1)} %shard_map.65.refs_0_), channel_id=1, source_target_pairs={{0,8},{1,9},{2,10},{3,11},{4,12},{5,13},{6,14},{7,15},{8,0},{9,1},... | collective-permute-start | bytes 3145736 | tf_op jit(solution)/shard_map/ppermute | solution.py:36
  73.2 25.1 %collective-permute-start.22 = (f32[256,1024]{1,0:T(8,128)S(1)}, f32[256,1024]{1,0:T(8,128)S(1)}, u32[]{:S(2)}, u32[]{:S(2)}) collective-permute-start(f32[256,1024]{1,0:T(8,128)S(1)} %shard_map.67.refs_6_.refs_8_), channel_id=1, source_target_pairs={{0,32},{1,97},{2,34},{3,99},{4,36},{5,101},{6,38},{7,103},{8,40},{... | collective-permute-start | bytes 3145736 | tf_op jit(solution)/shard_map/ppermute | solution.py:36
  75.6 25.8 %collective-permute-start.36 = (f32[256,1024]{1,0:T(8,128)S(1)}, f32[256,1024]{1,0:T(8,128)S(1)}, u32[]{:S(2)}, u32[]{:S(2)}) collective-permute-start(f32[256,1024]{1,0:T(8,128)S(1)} %shard_map.67.refs_6_.refs_8_), channel_id=1, source_target_pairs={{0,96},{1,33},{2,98},{3,35},{4,100},{5,37},{6,102},{7,39},{8,104},... | collective-permute-start | bytes 3145736 | tf_op jit(solution)/shard_map/ppermute | solution.py:36
  75.6 47.0 %collective-permute-start.19 = (f32[256,1024]{1,0:T(8,128)S(1)}, f32[256,1024]{1,0:T(8,128)S(1)}, u32[]{:S(2)}, u32[]{:S(2)}) collective-permute-start(f32[256,1024]{1,0:T(8,128)S(1)} %shard_map.67.refs_6_.refs_8_), channel_id=1, source_target_pairs={{0,16},{1,17},{2,18},{3,19},{4,20},{5,21},{6,22},{7,23},{8,24},{9,... | collective-permute-start | bytes 3145736 | tf_op jit(solution)/shard_map/ppermute | solution.py:36
  79.3 43.2 %collective-permute-start.33 = (f32[128,2048]{1,0:T(8,128)S(1)}, f32[128,2048]{1,0:T(8,128)S(1)}, u32[]{:S(2)}, u32[]{:S(2)}) collective-permute-start(f32[128,2048]{1,0:T(8,128)S(1)} %collective-permute-done.29.refs_1_), channel_id=1, source_target_pairs={{0,1},{1,0},{2,3},{3,2},{4,5},{5,4},{6,7},{7,6},{8,9},{9,8},{10,11... | collective-permute-start | bytes 3145736 | tf_op jit(solution)/shard_map/ppermute | solution.py:36
  97.0 26.4 %collective-permute-start.34 = (f32[128,2048]{1,0:T(8,128)S(1)}, f32[128,2048]{1,0:T(8,128)S(1)}, u32[]{:S(2)}, u32[]{:S(2)}) collective-permute-start(f32[128,2048]{1,0:T(8,128)S(1)} %collective-permute-done.30.refs_2_), channel_id=1, source_target_pairs={{0,1},{1,0},{2,3},{3,2},{4,5},{5,4},{6,7},{7,6},{8,9},{9,8},{10,11... | collective-permute-start | bytes 3145736 | tf_op jit(solution)/shard_map/ppermute | solution.py:36
  98.3 27.3 %collective-permute-start.31 = (f32[128,2048]{1,0:T(8,128)S(1)}, f32[128,2048]{1,0:T(8,128)S(1)}, u32[]{:S(2)}, u32[]{:S(2)}) collective-permute-start(f32[128,2048]{1,0:T(8,128)S(1)} %collective-permute-done.29.refs_1_), channel_id=1, source_target_pairs={{0,2},{1,7},{2,4},{3,1},{4,6},{5,3},{6,0},{7,5},{8,10},{9,15},{10,... | collective-permute-start | bytes 3145736 | tf_op jit(solution)/shard_map/ppermute | solution.py:36
  101.4 26.1 %collective-permute-start.25 = (f32[128,2048]{1,0:T(8,128)S(1)}, f32[128,2048]{1,0:T(8,128)S(1)}, u32[]{:S(2)}, u32[]{:S(2)}) collective-permute-start(f32[128,2048]{1,0:T(8,128)S(1)} %collective-permute-done.7.refs_0_), channel_id=1, source_target_pairs={{0,6},{1,3},{2,0},{3,5},{4,2},{5,7},{6,4},{7,1},{8,14},{9,11},{10,... | collective-permute-start | bytes 3145736 | tf_op jit(solution)/shard_map/ppermute | solution.py:36
  122.5 13.9 %collective-permute-start.8 = (f32[128,2048]{1,0:T(8,128)S(1)}, f32[128,2048]{1,0:T(8,128)S(1)}, u32[]{:S(2)}, u32[]{:S(2)}) collective-permute-start(f32[128,2048]{1,0:T(8,128)S(1)} %collective-permute-done.7.refs_0_), channel_id=1, source_target_pairs={{0,2},{1,7},{2,4},{3,1},{4,6},{5,3},{6,0},{7,5},{8,10},{9,15},{10,... | collective-permute-start | bytes 3145736 | tf_op jit(solution)/shard_map/ppermute | solution.py:36
  122.5 23.1 %collective-permute-start.26 = (f32[128,2048]{1,0:T(8,128)S(1)}, f32[128,2048]{1,0:T(8,128)S(1)}, u32[]{:S(2)}, u32[]{:S(2)}) collective-permute-start(f32[128,2048]{1,0:T(8,128)S(1)} %collective-permute-done.7.refs_0_), channel_id=1, source_target_pairs={{0,1},{1,0},{2,3},{3,2},{4,5},{5,4},{6,7},{7,6},{8,9},{9,8},{10,11... | collective-permute-start | bytes 3145736 | tf_op jit(solution)/shard_map/ppermute | solution.py:36
  123.4 22.4 %collective-permute-start.23 = (f32[256,1024]{1,0:T(8,128)S(1)}, f32[256,1024]{1,0:T(8,128)S(1)}, u32[]{:S(2)}, u32[]{:S(2)}) collective-permute-start(f32[256,1024]{1,0:T(8,128)S(1)} %collective-permute-done.22.refs_7_.refs_9_), channel_id=1, source_target_pairs={{0,32},{1,97},{2,34},{3,99},{4,36},{5,101},{6,38},{7,103},{8,40},{... | collective-permute-start | bytes 3145736 | tf_op jit(solution)/shard_map/ppermute | solution.py:36
  125.7 23.6 %collective-permute-start.20 = (f32[256,1024]{1,0:T(8,128)S(1)}, f32[256,1024]{1,0:T(8,128)S(1)}, u32[]{:S(2)}, u32[]{:S(2)}) collective-permute-start(f32[256,1024]{1,0:T(8,128)S(1)} %collective-permute-done.19.refs_4_.refs_6_.refs_2_), channel_id=1, source_target_pairs={{0,32},{1,97},{2,34},{3,99},{4,36},{5,101},{6,38},{7,103},{8,40},{... | collective-permute-start | bytes 3145736 | tf_op jit(solution)/shard_map/ppermute | solution.py:36
  127.5 23.9 %collective-permute-start.35 = (f32[128,2048]{1,0:T(8,128)S(1)}, f32[128,2048]{1,0:T(8,128)S(1)}, u32[]{:S(2)}, u32[]{:S(2)}) collective-permute-start(f32[128,2048]{1,0:T(8,128)S(1)} %collective-permute-done.31.refs_3_), channel_id=1, source_target_pairs={{0,1},{1,0},{2,3},{3,2},{4,5},{5,4},{6,7},{7,6},{8,9},{9,8},{10,11... | collective-permute-start | bytes 3145736 | tf_op jit(solution)/shard_map/ppermute | solution.py:36
  136.5 24.4 %collective-permute-start.9 = (f32[128,2048]{1,0:T(8,128)S(1)}, f32[128,2048]{1,0:T(8,128)S(1)}, u32[]{:S(2)}, u32[]{:S(2)}) collective-permute-start(f32[128,2048]{1,0:T(8,128)S(1)} %collective-permute-done.8.refs_1_), channel_id=1, source_target_pairs={{0,2},{1,7},{2,4},{3,1},{4,6},{5,3},{6,0},{7,5},{8,10},{9,15},{10,... | collective-permute-start | bytes 3145736 | tf_op jit(solution)/shard_map/ppermute | solution.py:36
  145.7 28.3 %collective-permute-start.21 = (f32[256,1024]{1,0:T(8,128)S(1)}, f32[256,1024]{1,0:T(8,128)S(1)}, u32[]{:S(2)}, u32[]{:S(2)}) collective-permute-start(f32[256,1024]{1,0:T(8,128)S(1)} %collective-permute-done.19.refs_4_.refs_6_.refs_2_), channel_id=1, source_target_pairs={{0,96},{1,33},{2,98},{3,35},{4,100},{5,37},{6,102},{7,39},{8,104},... | collective-permute-start | bytes 3145736 | tf_op jit(solution)/shard_map/ppermute | solution.py:36
  145.8 28.2 %collective-permute-start.27 = (f32[128,2048]{1,0:T(8,128)S(1)}, f32[128,2048]{1,0:T(8,128)S(1)}, u32[]{:S(2)}, u32[]{:S(2)}) collective-permute-start(f32[128,2048]{1,0:T(8,128)S(1)} %collective-permute-done.8.refs_1_), channel_id=1, source_target_pairs={{0,1},{1,0},{2,3},{3,2},{4,5},{5,4},{6,7},{7,6},{8,9},{9,8},{10,11... | collective-permute-start | bytes 3145736 | tf_op jit(solution)/shard_map/ppermute | solution.py:36
  149.3 24.8 %collective-permute-start.28 = (f32[128,2048]{1,0:T(8,128)S(1)}, f32[128,2048]{1,0:T(8,128)S(1)}, u32[]{:S(2)}, u32[]{:S(2)}) collective-permute-start(f32[128,2048]{1,0:T(8,128)S(1)} %collective-permute-done.25.refs_2_), channel_id=1, source_target_pairs={{0,1},{1,0},{2,3},{3,2},{4,5},{5,4},{6,7},{7,6},{8,9},{9,8},{10,11... | collective-permute-start | bytes 3145736 | tf_op jit(solution)/shard_map/ppermute | solution.py:36
  151.4 26.2 %collective-permute-start.24 = (f32[256,1024]{1,0:T(8,128)S(1)}, f32[256,1024]{1,0:T(8,128)S(1)}, u32[]{:S(2)}, u32[]{:S(2)}) collective-permute-start(f32[256,1024]{1,0:T(8,128)S(1)} %collective-permute-done.23.refs_11_), channel_id=1, source_target_pairs={{0,16},{1,17},{2,18},{3,19},{4,20},{5,21},{6,22},{7,23},{8,24},{9,... | collective-permute-start | bytes 3145736 | tf_op jit(solution)/shard_map/ppermute | solution.py:36
  160.9 24.8 %collective-permute-start.10 = (f32[128,2048]{1,0:T(8,128)S(1)}, f32[128,2048]{1,0:T(8,128)S(1)}, u32[]{:S(2)}, u32[]{:S(2)}) collective-permute-start(f32[128,2048]{1,0:T(8,128)S(1)} %collective-permute-done.9.refs_0_), channel_id=1, source_target_pairs={{0,1},{1,0},{2,3},{3,2},{4,5},{5,4},{6,7},{7,6},{8,9},{9,8},{10,11... | collective-permute-start | bytes 3145736 | tf_op jit(solution)/shard_map/ppermute | solution.py:36
  (16 other events, 117.0 us)
